TPU v7x, 256 devices: a whole 4x4x8 slice. The times are simulated.
256 devices in a mesh: space: 16 (over z_hi, x, core), freq: 16 (over y, z_lo).
Axes of the slice: x: 4, y: 4, z: 8 (z_hi: 2, z_lo: 4; z = z_hi * 4 + z_lo), core: 2. Of those that a mesh axis runs over, the one named last changes fastest.
Arguments:
- spectrum: float32 [32, 36, 512, 256], P('freq', None, 'space'), may hold values from 0.05 to 2
- land_sea: int32 [512, 256], P('space'), may hold values 0 or 1
- courant: float32 [32], P('freq'), may hold values from 0.2 to 0.65
- refract: float32 [32], P('freq'), may hold values from 0.2 to 0.9
- depth_dx: float32 [512, 256], P('space'), may hold values from -0.5 to 0.5
- depth_dy: float32 [512, 256], P('space'), may hold values from -0.5 to 0.5
- w_in: bfloat16 [1152, 2048], P(None, 'freq'), may hold values from -0.1875 to 0.1875
- w_out: bfloat16 [2048, 1152], P('freq'), may hold values from -0.125 to 0.125
Outputs:
- spectrum_out: float32 [32, 36, 512, 256], P('freq', None, 'space')
All inputs are finite; a program needn't handle non-finite values. No bound on the sum of `land_sea` on one device may be relied on, other than what follows from the above.
Results may differ from a plain program's by a relative error of at most 0.003.
Values may be sent and summed in bfloat16 or wider, within the bound.
A program may use at most 128 MiB of HBM per device.

v0:
```python
import math

import jax
import jax.numpy as jnp
from jax import lax
from jax.sharding import PartitionSpec as P

DIRS = 36
STEPS = 2


step_scale = 0.5
epsilon = 1e-06


def rows_first(arrays, axis, dims):
    turned = [jnp.moveaxis(a, dim, 0) for a, dim in zip(arrays, dims)]
    widths = [t[0].size for t in turned]
    both = jnp.concatenate([t.reshape(-1, w) for t, w in zip(turned, widths)], axis=1)
    out = lax.all_gather(both, axis, axis=0, tiled=True)
    parts = jnp.split(out, [sum(widths[:k]) for k in range(1, len(widths))], axis=1)
    return tuple(
        (
            jnp.moveaxis(b.reshape(-1, *t.shape[1:]), 0, dim)
            for b, t, dim in zip(parts, turned, dims)
        )
    )


def padded_2(block, sides, width):
    for axis, dim in sides:
        count = lax.axis_size(axis)
        forward = [(i, i + 1) for i in range(count - 1)]
        backward = [(target, source) for source, target in forward]
        low = lax.ppermute(
            lax.slice_in_dim(block, block.shape[dim] - width, None, axis=dim), axis, forward
        )
        high = lax.ppermute(lax.slice_in_dim(block, 0, width, axis=dim), axis, backward)
        block = jnp.concatenate([low, block, high], axis=dim)
    return block


def sent_to_all(shard, axis):
    copies = jnp.broadcast_to(shard, (lax.axis_size(axis), *shard.shape))
    return lax.all_to_all(copies, axis, split_axis=0, concat_axis=0, tiled=True)


def over_copies(shard, axis):
    everything = sent_to_all(shard, axis)
    return jnp.sum(everything, axis=0)


def direction_tables():
    angles = (jnp.arange(DIRS, dtype=jnp.float32) + 0.5) * (2.0 * math.pi / DIRS)
    return (jnp.cos(angles), jnp.sin(angles))


def transport(padded, courant, refract, depth_dx, depth_dy, seamask):
    cosine, sine_dir = direction_tables()
    speed_x = courant[:, None] * cosine[None, :]
    speed_y = courant[:, None] * sine_dir[None, :]
    pos_x = jnp.maximum(speed_x, 0.0)[:, :, None, None]
    neg_x = jnp.maximum(-speed_x, 0.0)[:, :, None, None]
    pos_y = jnp.maximum(speed_y, 0.0)[:, :, None, None]
    neg_y = jnp.maximum(-speed_y, 0.0)[:, :, None, None]
    center = padded[:, :, 1:-1, 1:-1]
    keeping = 1.0 - jnp.abs(speed_x)[:, :, None, None] - jnp.abs(speed_y)[:, :, None, None]
    shifted = center * keeping + pos_x * padded[:, :, :-2, 1:-1] + neg_x * padded[:, :, 2:, 1:-1]
    shifted = shifted + pos_y * padded[:, :, 1:-1, :-2] + neg_y * padded[:, :, 1:-1, 2:]
    turn_rate = refract[:, None, None, None] * (
        sine_dir[None, :, None, None] * depth_dx[None, None]
        - cosine[None, :, None, None] * depth_dy[None, None]
    )
    turn_pos = jnp.maximum(turn_rate, 0.0)
    turn_neg = jnp.maximum(-turn_rate, 0.0)
    turned = shifted * (1.0 - jnp.abs(turn_rate)) + jnp.roll(turn_pos * shifted, 1, axis=1)
    turned = turned + jnp.roll(turn_neg * shifted, -1, axis=1)
    return turned * seamask[None, None]


def body(spectrum, land_sea, courant, refract, depth_dx, depth_dy, w_in, w_out):
    contract = (((0,), (0,)), ((), ()))
    seamask = land_sea.astype(jnp.float32)
    groups = lax.axis_size("freq")
    local_freqs, directions, rows, columns = spectrum.shape
    point_rows = rows // groups
    channels = local_freqs * groups * directions
    in_whole, out_whole = rows_first((w_in, w_out), "freq", (1, 0))
    field = spectrum
    for repeat in range(STEPS):
        padded = padded_2(field, (("space", 2),), 1)
        padded = jnp.pad(padded, ((0, 0), (0, 0), (0, 0), (1, 1)))
        field = transport(padded, courant, refract, depth_dx, depth_dy, seamask)
        partial_sum = jnp.sum(field, axis=(0, 1))
        point_total = over_copies(partial_sum, "freq")
        energy_mean = point_total / channels + epsilon
        scaled = (field / energy_mean[None, None]).astype(jnp.bfloat16)
        arrived = lax.all_to_all(scaled, "freq", split_axis=2, concat_axis=0, tiled=True)
        preact = lax.dot_general(
            in_whole,
            arrived.reshape(channels, point_rows * columns),
            contract,
            preferred_element_type=jnp.float32,
        )
        hidden = jax.nn.gelu(preact).astype(jnp.bfloat16)
        source = lax.dot_general(out_whole, hidden, contract, preferred_element_type=jnp.float32)
        source = source.astype(jnp.bfloat16)
        shaped = source.reshape(local_freqs * groups, directions, point_rows, columns)
        returned = lax.all_to_all(shaped, "freq", split_axis=0, concat_axis=2, tiled=True)
        field = field * jnp.exp(step_scale * jnp.tanh(returned.astype(jnp.float32)))
    return field


def solution(mesh):
    placed = (
        P("freq", None, "space", None),
        P("space", None),
        P("freq"),
        P("freq"),
        P("space", None),
        P("space", None),
        P(None, "freq"),
        P("freq", None),
    )
    return jax.shard_map(
        body, mesh=mesh, in_specs=placed, out_specs=P("freq", None, "space", None), check_vma=False
    )
```

profile of v0, /device:TPU:1, one launch (start us, length us, event | category | flops | bytes accessed | tf_op | source)
XLA Modules:
  0.0 445.0 jit_solution(3706693780660237277)
XLA Ops:
  6.5 1.2 copy.49
  7.7 1.8 pad_maximum_fusion.4
  9.6 1.4 fusion.85
  10.9 5.1 %collective-permute-start.1 = (f32[2,36,1,256]{3,1,2,0:T(8,128)S(1)}, f32[2,36,1,256]{3,1,2,0:T(8,128)S(1)}, u32[]{:S(2)}, u32[]{:S(2)}) collective-permute-start(f32[2,36,1,256]{3,1,2,0:T(8,128)S(1)} %copy.62), channel_id=1, source_target_pairs={{16,0},{32,16},{48,32},{64,48},{80,64},{96,80},{112,96},{128,112},... | collective-permute-start | bytes 221192 | tf_op jit(solution)/shard_map/ppermute | solution.py:38
  16.1 1.9 collective-permute-start
  18.4 3.0 copy.39
  21.5 1.1 select_maximum_fusion.2
  22.6 2.1 fusion.44
  25.7 2.8 fusion.82
  28.6 38.5 %all_to_all.58 = f32[16,32,256]{2,1,0:T(8,128)S(1)} all-to-all(f32[16,32,256]{2,1,0:T(8,128)S(1)} %broadcast_in_dim.4), channel_id=1, replica_groups=mesh['space'=16,'freq'=16] {'freq'}, dimensions={0} | all-to-all | bytes 1048576 | tf_op jit(solution)/shard_map/all_to_all | solution.py:45
  67.1 2.0 divide_convert_fusion.1
  69.2 72.5 %all_to_all.59 = bf16[2,36,32,256]{3,1,0,2:T(8,128)(2,1)S(1)} all-to-all(bf16[2,36,32,256]{3,1,0,2:T(8,128)(2,1)S(1)} %divide_convert_fusion.1), channel_id=1, replica_groups=mesh['space'=16,'freq'=16] {'freq'}, dimensions={2} | all-to-all | bytes 2359296 | tf_op jit(solution)/shard_map/all_to_all | solution.py:98
  142.9 110.4 %all-gather.2.cloned.1.call-done = bf16[2048,2304]{1,0:T(8,128)(2,1)} async-done(((bf16[128,2304]{1,0:T(8,128)(2,1)}), bf16[2048,2304]{1,0:T(8,128)(2,1)}) %all-gather.2.cloned.1.call-update) | async-done | bytes 9437200 | tf_op jit(solution)/shard_map/all_gather | solution.py:20
  253.3 10.5 %fusion.27 = bf16[1152,512]{1,0:T(8,128)(2,1)} fusion(bf16[2048,2304]{1,0:T(8,128)(2,1)} %all-gather.2.cloned.1.call-done, bf16[1152,512]{1,0:T(8,128)(2,1)S(1)} %bitcast.45), kind=kOutput, calls=%fused_computation.38 | convolution fusion | flops 4841865216 | bytes 11796480 | tf_op jit(solution)/shard_map/dot_general | solution.py:106
  263.8 2.9 reshape.239
  266.7 37.9 %all_to_all.60 = bf16[32,36,2,256]{3,2,1,0:T(2,128)(2,1)S(1)} all-to-all(bf16[32,36,2,256]{3,2,1,0:T(2,128)(2,1)S(1)} %reshape.239), channel_id=1, replica_groups=mesh['space'=16,'freq'=16] {'freq'}, dimensions={0} | all-to-all | bytes 2359296 | tf_op jit(solution)/shard_map/all_to_all | solution.py:109
  304.6 2.4 multiply_exponential_fusion.1
  307.4 1.4 copy-done
  309.4 4.4 collective-permute-start.2
  313.8 2.1 collective-permute-start.3
  315.9 3.6 collective-permute-done.3
  320.7 2.1 fusion.43
  323.8 2.8 fusion.79
  326.6 17.7 %all_to_all.61 = f32[16,32,256]{2,1,0:T(8,128)S(1)} all-to-all(f32[16,32,256]{2,1,0:T(8,128)S(1)} %broadcast_in_dim.5), channel_id=1, replica_groups=mesh['space'=16,'freq'=16] {'freq'}, dimensions={0} | all-to-all | bytes 1048576 | tf_op jit(solution)/shard_map/all_to_all | solution.py:45
  344.3 2.0 divide_convert_fusion
  346.4 35.4 %all_to_all.62 = bf16[2,36,32,256]{3,1,0,2:T(8,128)(2,1)S(1)} all-to-all(bf16[2,36,32,256]{3,1,0,2:T(8,128)(2,1)S(1)} %divide_convert_fusion), channel_id=1, replica_groups=mesh['space'=16,'freq'=16] {'freq'}, dimensions={2} | all-to-all | bytes 2359296 | tf_op jit(solution)/shard_map/all_to_all | solution.py:98
  382.9 10.5 %fusion.30 = bf16[1152,512]{1,0:T(8,128)(2,1)} fusion(bf16[2048,2304]{1,0:T(8,128)(2,1)} %all-gather.2.cloned.1.call-done, bf16[1152,512]{1,0:T(8,128)(2,1)S(1)} %bitcast.46), kind=kOutput, calls=%fused_computation.39 | convolution fusion | flops 4841865216 | bytes 11796480 | tf_op jit(solution)/shard_map/dot_general | solution.py:106
  393.4 2.9 reshape.241
  396.3 34.1 %all_to_all.63 = bf16[32,36,2,256]{3,2,1,0:T(2,128)(2,1)S(1)} all-to-all(bf16[32,36,2,256]{3,2,1,0:T(2,128)(2,1)S(1)} %reshape.241), channel_id=1, replica_groups=mesh['space'=16,'freq'=16] {'freq'}, dimensions={0} | all-to-all | bytes 2359296 | tf_op jit(solution)/shard_map/all_to_all | solution.py:109
  430.5 2.4 multiply_exponential_fusion
  433.3 1.4 copy-done.1
  435.1 2.8 copy.60
  (47 shorter events, 7.7 us)
Async XLA Ops:
  6.5 11.5 %copy-start.2 = (f32[32,256]{1,0:T(8,128)S(1)}, f32[32,256]{1,0:T(8,128)}, u32[]{:S(2)}) copy-start(f32[32,256]{1,0:T(8,128)} %param.13) | copy-start | bytes 98308
  6.5 11.5 %copy-start.3 = (f32[32,256]{1,0:T(8,128)S(1)}, f32[32,256]{1,0:T(8,128)}, u32[]{:S(2)}) copy-start(f32[32,256]{1,0:T(8,128)} %param.12) | copy-start | bytes 98308
  6.5 11.8 %copy-start.6 = (f32[2]{0:T(128)S(1)}, f32[2]{0:T(128)}, u32[]{:S(2)}) copy-start(f32[2]{0:T(128)} %param.10) | copy-start | bytes 28
  6.5 246.8 %all-gather.2.cloned.1.call-start = ((), (), s32[]{:S(2)}) async-start(), calls=%async_computation.6 | async-start | bytes 10027008 | tf_op jit(solution)/shard_map/all_gather | solution.py:20
  10.9 10.5 %collective-permute-start.1 = (f32[2,36,1,256]{3,1,2,0:T(8,128)S(1)}, f32[2,36,1,256]{3,1,2,0:T(8,128)S(1)}, u32[]{:S(2)}, u32[]{:S(2)}) collective-permute-start(f32[2,36,1,256]{3,1,2,0:T(8,128)S(1)} %copy.62), channel_id=1, source_target_pairs={{16,0},{32,16},{48,32},{64,48},{80,64},{96,80},{112,96},{128,112},... | collective-permute-start | bytes 221192 | tf_op jit(solution)/shard_map/ppermute | solution.py:38
  16.1 5.4 %collective-permute-start = (f32[2,36,1,256]{3,1,2,0:T(8,128)S(1)}, f32[2,36,1,256]{3,1,2,0:T(8,128)S(1)}, u32[]{:S(2)}, u32[]{:S(2)}) collective-permute-start(f32[2,36,1,256]{3,1,2,0:T(8,128)S(1)} %copy.61), channel_id=1, source_target_pairs={{0,16},{16,32},{32,48},{48,64},{64,80},{80,96},{96,112},{112,128},... | collective-permute-start | bytes 221192 | tf_op jit(solution)/shard_map/ppermute | solution.py:35
  18.3 3.1 copy-start.4
  21.5 1.2 copy-start.5
  307.1 1.7 copy-start
  309.4 6.5 %collective-permute-start.2 = (f32[2,36,1,256]{3,1,2,0:T(8,128)S(1)}, f32[2,36,1,256]{3,1,2,0:T(8,128)S(1)}, u32[]{:S(2)}, u32[]{:S(2)}) collective-permute-start(f32[2,36,1,256]{3,1,2,0:T(8,128)S(1)} %get-tuple-element.13), channel_id=1, source_target_pairs={{0,16},{16,32},{32,48},{48,64},{64,80},{80,96},{96,112},{112,128},... | collective-permute-start | bytes 221192 | tf_op jit(solution)/shard_map/ppermute | solution.py:35
  313.8 5.8 %collective-permute-start.3 = (f32[2,36,1,256]{3,1,2,0:T(8,128)S(1)}, f32[2,36,1,256]{3,1,2,0:T(8,128)S(1)}, u32[]{:S(2)}, u32[]{:S(2)}) collective-permute-start(f32[2,36,1,256]{3,1,2,0:T(8,128)S(1)} %get-tuple-element.14), channel_id=1, source_target_pairs={{16,0},{32,16},{48,32},{64,48},{80,64},{96,80},{112,96},{128,112},... | collective-permute-start | bytes 221192 | tf_op jit(solution)/shard_map/ppermute | solution.py:38
  432.9 1.7 copy-start.1
Sparse Core Ops, SparseCore 0:
  9.7 243.5 all-gather.1
where the time goes:
time: 453 us; the launch traced here: 445 us
  blocking collectives  236 us (52%)
  waiting for transfers between devices  114 us (25%)
  other arithmetic  25.3 us (6%)
  local copies, waits for them, and re-layouts  21 us (5%)
  matrix products  20.9 us (5%)
  between operations  14 us (3%)
  starting transfers between devices  13.5 us (3%)
    all_gather x1, waiting for transfers between devices, rows_first(): out = lax.all_gather(both, axis, axis=0, tiled=True)  110 us
    all_to_all x2, blocking collectives, body(): lax.all_to_all(scaled, 'freq', split_axis=2, concat_axis=0, tiled=True)  108 us
    all_to_all x2, blocking collectives, body(): lax.all_to_all(shaped, 'freq', split_axis=0, concat_axis=2, tiled=True)  72 us
    all_to_all x2, blocking collectives, sent_to_all(): return lax.all_to_all(copies, axis, split_axis=0, concat_axis=0, tiled=True)  56.2 us
    dot_general x2, matrix products, body(): lax.dot_general(out_whole, hidden, contract, preferred_element_type=jnp.f...  20.9 us
  transfers between devices with their start and end apart: 5, of which 2 were waited for; matrix products, arithmetic and copies ran while one was open for 3% of the time, Pallas kernels for 0%

commit v1 on v0

v1 whole, which is shorter than its diff:
```python
import math

import jax
import jax.numpy as jnp
from jax import lax
from jax.experimental import pallas as pl
from jax.experimental.pallas import tpu as pltpu
from jax.sharding import PartitionSpec as P

DIRS = 36
MESH = pl.DeviceIdType.MESH

step_scale = 0.5
epsilon = 1e-06

TOP_T1 = 2.45
TOP_E1 = 4.06
TOP_E2 = 8.2
LEVELS = 65535.0
HALF = 32768.0


def encode(value, top):
    level = jnp.minimum(value * (LEVELS / top) + 0.5, LEVELS)
    return (level.astype(jnp.int32) - 32768).astype(jnp.int16)


def decode(code, top):
    return (code.astype(jnp.int32).astype(jnp.float32) + HALF) * (top / LEVELS)


def freq_of(j):
    zl = j // 4
    yy = j % 4
    return (yy + (zl % 2) * (3 - 2 * yy)) * 4 + zl


def place_of(f):
    y = f // 4
    zl = f % 4
    return zl * 4 + y + (zl % 2) * (3 - 2 * y)


def coefficients(table, cosine, sine):
    first = lax.broadcasted_iota(jnp.int32, cosine.shape, 0) < DIRS
    courant = jnp.where(first, table[0:1], table[1:2])
    refract = jnp.where(first, table[2:3], table[3:4])
    speed_x = courant * cosine
    speed_y = courant * sine
    pos_x = jnp.maximum(speed_x, 0.0)
    pos_y = jnp.maximum(speed_y, 0.0)
    keep = 1.0 - jnp.abs(speed_x) - jnp.abs(speed_y)
    return keep, pos_x, pos_x - speed_x, pos_y, pos_y - speed_y, refract * sine, refract * cosine


def transport_row(before, center, after, coef, dx, dy, sea):
    keep, pos_x, neg_x, pos_y, neg_y, turn_x, turn_y = coef
    rows, cols = center.shape
    lane = lax.broadcasted_iota(jnp.int32, center.shape, 1)
    west = jnp.where(lane == 0, 0.0, pltpu.roll(center, 1, 1))
    east = jnp.where(lane == cols - 1, 0.0, pltpu.roll(center, cols - 1, 1))
    shifted = center * keep + pos_x * before + neg_x * after + pos_y * west + neg_y * east
    turning = (turn_x * dx - turn_y * dy) * shifted
    moved_up = jnp.maximum(turning, 0.0)
    moved_down = jnp.maximum(-turning, 0.0)
    d = lax.broadcasted_iota(jnp.int32, center.shape, 0)
    lower = jnp.where((d == 0) | (d == DIRS), pltpu.roll(moved_up, DIRS + 1, 0), pltpu.roll(moved_up, 1, 0))
    upper = jnp.where(
        (d == DIRS - 1) | (d == rows - 1),
        pltpu.roll(moved_down, DIRS - 1, 0),
        pltpu.roll(moved_down, rows - 1, 0),
    )
    return (shifted - jnp.abs(turning) + lower + upper) * sea


def gelu(x):
    return 0.5 * x * (1.0 + jnp.tanh(math.sqrt(2.0 / math.pi) * (x + 0.044715 * x * x * x)))


def kernel(
    field, dx, dy, sea, cos_ref, sin_ref, own_table, own_w, out,
    weights, codes1, got1, codes2, got2, table, edge_out, edge_in, energy, moved, x_buf, h_buf, s_buf, coef_buf,
    z_send, z_recv, y_send, y_recv, x_send, x_recv, d_send, d_recv, a_send, a_recv, t_send, t_recv,
    e_send, e_recv, b_send, b_recv, local_sem,
):
    s = lax.axis_index("space")
    f = lax.axis_index("freq")
    core = s % 2
    x = (s // 2) % 4
    base = (s // 8) * 8
    y = f // 4
    zl = f % 4
    j = place_of(f)
    chans = field.shape[1]
    cols = field.shape[2]
    groups = 16

    def at_freq(g):
        return {"space": s, "freq": g}

    def at_x(step):
        return {"space": base + ((x + step) % 4) * 2 + core, "freq": f}

    partner = {"space": s + 1 - 2 * core, "freq": f}
    has_up = jnp.logical_or(j > 0, s > 0)
    has_down = jnp.logical_or(j < 15, s < 15)
    up = {"space": jnp.where(j > 0, s, jnp.maximum(s - 1, 0)), "freq": freq_of((j + 15) % 16)}
    down = {"space": jnp.where(j < 15, s, jnp.minimum(s + 1, 15)), "freq": freq_of((j + 1) % 16)}

    barrier = pltpu.get_barrier_semaphore()
    for k in range(1, groups):
        pl.semaphore_signal(barrier, inc=1, device_id=at_freq((f + k) % 16), device_id_type=MESH)
    pl.semaphore_signal(barrier, inc=1, device_id=at_x(1), device_id_type=MESH)
    pl.semaphore_signal(barrier, inc=1, device_id=at_x(3), device_id_type=MESH)
    pl.semaphore_signal(barrier, inc=1, device_id=partner, device_id_type=MESH)
    over_top = jnp.logical_and(j == 0, s > 0)
    over_bottom = jnp.logical_and(j == 15, s < 15)

    @pl.when(over_top)
    def _():
        pl.semaphore_signal(barrier, inc=1, device_id=up, device_id_type=MESH)

    @pl.when(over_bottom)
    def _():
        pl.semaphore_signal(barrier, inc=1, device_id=down, device_id_type=MESH)

    pl.semaphore_wait(barrier, 18 + over_top.astype(jnp.int32) + over_bottom.astype(jnp.int32))

    def remote(src, dst, send, recv, target):
        return pltpu.make_async_remote_copy(
            src_ref=src, dst_ref=dst, send_sem=send, recv_sem=recv, device_id=target, device_id_type=MESH
        )

    def quarter(q):
        return pl.ds(pl.multiple_of(q * 32, 32), 32)

    own_quarter = weights.at[core, f, :, quarter(x), :]
    place = pltpu.make_async_copy(own_w.at[core, :, quarter(x), :], own_quarter, local_sem.at[0])
    place.start()
    place.wait()
    z_copies = []
    for k in range(1, 4):
        c = remote(own_quarter, own_quarter, z_send.at[k - 1], z_recv.at[k - 1], at_freq(y * 4 + (zl + k) % 4))
        c.start()
        z_copies.append(c)
    table[f] = own_table[...]
    t_copies = []
    for k in range(1, groups):
        c = remote(own_table, table.at[f], t_send.at[k], t_recv.at[k], at_freq((f + k) % 16))
        c.start()
        t_copies.append(c)

    def y_block(r, first=0, count=4, q=x):
        return weights.at[core, pl.ds(r * 4 + first, count), :, quarter(q), :]

    y_right, y_left = at_freq(((y + 1) % 4) * 4 + zl), at_freq(((y + 3) % 4) * 4 + zl)
    order = [y, (y + 3) % 4, (y + 1) % 4, (y + 2) % 4]
    xs = [x, (x + 3) % 4, (x + 1) % 4, (x + 2) % 4]
    y_copies, x_copies, d_copies = {}, {}, {}

    def go(where, key, copy):
        copy.start()
        where[key] = copy

    def spread(b):
        r = order[b]
        block = y_block(r)
        go(x_copies, (b, 0), remote(block, block, x_send.at[b, 0], x_recv.at[b, 0], at_x(1)))
        go(x_copies, (b, 1), remote(block, block, x_send.at[b, 1], x_recv.at[b, 1], at_x(3)))
        share(b, 0)

    def share(b, k):
        block = y_block(order[b], q=xs[k])
        go(d_copies, (b, k), remote(block, block, d_send.at[b, k], d_recv.at[b, k], partner))

    def weights_1():
        for c in z_copies:
            c.wait_recv()
        own = y_block(y)
        go(y_copies, 0, remote(own, own, y_send.at[0], y_recv.at[0], y_right))
        go(y_copies, 1, remote(own, own, y_send.at[1], y_recv.at[1], y_left))
        spread(0)

    def weights_2():
        y_copies[0].wait_recv()
        part = y_block(order[1], 0, 2)
        go(y_copies, 2, remote(part, part, y_send.at[2], y_recv.at[2], y_right))
        spread(1)

    def weights_3():
        y_copies[1].wait_recv()
        part = y_block(order[2], 2, 2)
        go(y_copies, 3, remote(part, part, y_send.at[3], y_recv.at[3], y_left))
        spread(2)

    def weights_4():
        y_copies[2].wait_recv()
        y_copies[3].wait_recv()
        spread(3)

    def weights_5(b):
        x_copies[b, 0].wait_recv()
        part = y_block(order[b], 0, 2, xs[1])
        go(x_copies, (b, 2), remote(part, part, x_send.at[b, 2], x_recv.at[b, 2], at_x(1)))
        share(b, 1)
        x_copies[b, 1].wait_recv()
        part = y_block(order[b], 2, 2, xs[2])
        go(x_copies, (b, 3), remote(part, part, x_send.at[b, 3], x_recv.at[b, 3], at_x(3)))
        share(b, 2)

    def weights_6(b):
        x_copies[b, 2].wait_recv()
        x_copies[b, 3].wait_recv()
        share(b, 3)

    coef = coefficients(own_table[...], cos_ref[...], sin_ref[...])
    for i, c in enumerate(coef):
        coef_buf[i] = c

    def first_rows(k, carry):
        jj = (j + k) % 16
        for r in range(2):
            row = jj * 2 + r
            value = transport_row(
                field[row], field[row + 1], field[row + 2], [coef_buf[i] for i in range(7)], dx[row], dy[row], sea[row]
            )
            codes1[jj, r] = encode(value, TOP_T1)
        return carry

    a_copies = []
    hooks = {3: weights_1, 7: weights_2, 9: weights_3, 12: weights_4}

    def send_rows(k):
        jj = (j + k) % 16
        c = remote(codes1.at[jj], got1.at[f], a_send.at[k], a_recv.at[k], at_freq(freq_of(jj)))
        c.start()
        a_copies.append(c)

    def first_and_send(k, carry):
        first_rows(k, carry)
        jj = (j + k) % 16
        remote(codes1.at[jj], got1.at[f], a_send.at[k], a_recv.at[jj * 0 + k], at_freq(freq_of(jj))).start()
        return carry

    bounds = [1, 4, 7, 10, 13, 16]
    steps = [weights_1, weights_2, weights_3, weights_4, None]
    for n in range(5):
        lax.fori_loop(bounds[n], bounds[n + 1], first_and_send, 0)
        if steps[n] is not None:
            steps[n]()
    first_rows(0, 0)
    mine = pltpu.make_async_copy(codes1.at[j], got1.at[f], local_sem.at[0])
    mine.start()
    mine.wait()
    for b in range(4):
        weights_5(b)

    def await_rows(k, carry):
        g = freq_of((j + 16 - k) % 16)
        remote(codes1.at[0], got1.at[g], a_send.at[k], a_recv.at[k], at_freq(g)).wait_recv()
        return carry

    lax.fori_loop(1, 16, await_rows, 0)
    for b in range(4):
        weights_6(b)
    for c in d_copies.values():
        c.wait_recv()

    def network():
        def first_layer(i, carry):
            lhs = jnp.concatenate(
                [
                    jnp.concatenate([weights[0, i * 4 + q, k] for k in range(9)], axis=1)
                    for q in range(4)
                ],
                axis=0,
            )
            pre = jnp.dot(lhs, x_buf[...], preferred_element_type=jnp.float32)
            h_buf[pl.ds(pl.multiple_of(i * 512, 512), 512), :] = gelu(pre).astype(jnp.bfloat16)
            return carry

        lax.fori_loop(0, 4, first_layer, 0)

        def second_layer(i, carry):
            lhs = jnp.concatenate(
                [
                    jnp.concatenate([weights[1, g, i * 3 + k] for g in range(16)], axis=1)
                    for k in range(3)
                ],
                axis=0,
            )
            s_buf[pl.ds(pl.multiple_of(i * 384, 384), 384), :] = jnp.dot(
                lhs, h_buf[...], preferred_element_type=jnp.float32
            )
            return carry

        lax.fori_loop(0, 3, second_layer, 0)

    def scale_into_x(total):
        mean = jnp.sum(total, axis=0, keepdims=True) * (1.0 / 1152.0) + epsilon
        inverse = 1.0 / mean

        def pair(p, carry):
            both = jnp.concatenate([moved[p * 2], moved[p * 2 + 1]], axis=0) * inverse
            x_buf[pl.ds(pl.multiple_of(p * 144, 144), 144), :] = both.astype(jnp.bfloat16)
            return carry

        lax.fori_loop(0, 8, pair, 0)

    def growth(g):
        return jnp.exp(step_scale * jnp.tanh(s_buf[pl.ds(pl.multiple_of(g * 72, 8), 72), :]))

    zeros = jnp.zeros((chans, cols), jnp.float32)
    edge_copies = []
    for r in range(2):

        def load(g, total):
            value = decode(got1[g, r], TOP_T1)
            moved[g] = value
            return total + value

        scale_into_x(lax.fori_loop(0, groups, load, zeros))
        network()

        def update(g, carry):
            value = moved[g] * growth(g)
            energy[g, r + 1] = value
            edge_out[r, g] = encode(value, TOP_E1)
            return carry

        lax.fori_loop(0, groups, update, 0)
        c = remote(edge_out.at[r], edge_in.at[1 - r], e_send.at[r], e_recv.at[1 - r], up if r == 0 else down)
        edge_copies.append(c)
        pl.when(has_up if r == 0 else has_down)(c.start)

    for k in range(1, groups):
        t_copies[k - 1].wait_recv()

    @pl.when(has_up)
    def _():
        edge_copies[1].wait_recv()

        def fill(g, carry):
            energy[g, 0] = decode(edge_in[0, g], TOP_E1)
            return carry

        lax.fori_loop(0, groups, fill, 0)

    @pl.when(jnp.logical_not(has_up))
    def _():
        def fill(g, carry):
            energy[g, 0] = zeros
            return carry

        lax.fori_loop(0, groups, fill, 0)

    @pl.when(has_down)
    def _():
        edge_copies[0].wait_recv()

        def fill(g, carry):
            energy[g, 3] = decode(edge_in[1, g], TOP_E1)
            return carry

        lax.fori_loop(0, groups, fill, 0)

    @pl.when(jnp.logical_not(has_down))
    def _():
        def fill(g, carry):
            energy[g, 3] = zeros
            return carry

        lax.fori_loop(0, groups, fill, 0)

    for r in range(2):
        row = j * 2 + r

        def second(g, total):
            coef = coefficients(table[g], cos_ref[...], sin_ref[...])
            value = transport_row(energy[g, r], energy[g, r + 1], energy[g, r + 2], coef, dx[row], dy[row], sea[row])
            moved[g] = value
            return total + value

        scale_into_x(lax.fori_loop(0, groups, second, zeros))
        network()

        def finish(k, carry):
            g = (f + k) % 16
            codes2[g, r] = encode(moved[g] * growth(g), TOP_E2)
            return carry

        def finish_and_send(k, carry):
            finish(k, carry)
            g = (f + k) % 16
            remote(codes2.at[g, r], got2.at[j, r], b_send.at[r, k], b_recv.at[r, k], at_freq(g)).start()
            return carry

        lax.fori_loop(1, groups, finish_and_send, 0)
        finish(0, 0)

    own_back = pltpu.make_async_copy(codes2.at[f], got2.at[j], local_sem.at[0])
    own_back.start()
    own_back.wait()

    def await_back(k, carry):
        g = (f + 16 - k) % 16
        for r in range(2):
            remote(codes2.at[0, 0], got2.at[place_of(g), r], b_send.at[r, k], b_recv.at[r, k], at_freq(g)).wait_recv()
        return carry

    lax.fori_loop(1, groups, await_back, 0)

    def put(row, carry):
        out[row * 2] = got2[row, 0]
        out[row * 2 + 1] = got2[row, 1]
        return carry

    lax.fori_loop(0, groups, put, 0)

    for c in z_copies + t_copies + list(y_copies.values()) + list(x_copies.values()) + list(d_copies.values()):
        c.wait_send()

    def sent(k, carry):
        remote(codes1.at[0], got1.at[0], a_send.at[k], a_recv.at[k], partner).wait_send()
        for r in range(2):
            remote(codes2.at[0, 0], got2.at[0, 0], b_send.at[r, k], b_recv.at[r, k], partner).wait_send()
        return carry

    lax.fori_loop(1, groups, sent, 0)
    for r in range(2):
        pl.when(has_up if r == 0 else has_down)(edge_copies[r].wait_send)


def direction_tables():
    angles = (jnp.arange(DIRS, dtype=jnp.float32) + 0.5) * (2.0 * math.pi / DIRS)
    return (jnp.cos(angles), jnp.sin(angles))


def body(spectrum, land_sea, courant, refract, depth_dx, depth_dy, w_in, w_out):
    freqs, dirs, rows, cols = spectrum.shape
    chans = freqs * dirs
    count = lax.axis_size("space")
    forward = [(i, i + 1) for i in range(count - 1)]
    backward = [(b, a) for a, b in forward]
    low = lax.ppermute(spectrum[:, :, rows - 1 :], "space", forward)
    high = lax.ppermute(spectrum[:, :, :1], "space", backward)
    padded = jnp.concatenate([low, spectrum, high], axis=2).reshape(chans, rows + 2, cols)
    field = jnp.transpose(padded, (1, 0, 2))
    cosine, sine = direction_tables()
    cos_table = jnp.broadcast_to(jnp.tile(cosine, freqs)[:, None], (chans, cols))
    sin_table = jnp.broadcast_to(jnp.tile(sine, freqs)[:, None], (chans, cols))
    own_table = jnp.concatenate([courant, refract, jnp.zeros((4,), jnp.float32)])
    own_table = jnp.broadcast_to(own_table[:, None], (8, cols))
    first = jnp.transpose(w_in.reshape(9, 128, 128), (0, 2, 1))
    second = jnp.transpose(w_out.reshape(128, 9, 128), (1, 2, 0))
    own_w = jnp.stack([first, second])

    def line(a):
        return a.astype(jnp.float32).reshape(rows, 1, cols)

    vmem = pl.BlockSpec(memory_space=pltpu.VMEM)
    dma = pltpu.SemaphoreType.DMA
    i16, f32, b16 = jnp.int16, jnp.float32, jnp.bfloat16
    back = pl.pallas_call(
        kernel,
        out_shape=jax.ShapeDtypeStruct((rows, chans, cols), i16),
        in_specs=[vmem] * 8,
        out_specs=vmem,
        scratch_shapes=[
            pltpu.VMEM((2, 16, 9, 128, 128), b16),
            pltpu.VMEM((16, 2, chans, cols), i16),
            pltpu.VMEM((16, 2, chans, cols), i16),
            pltpu.VMEM((16, 2, chans, cols), i16),
            pltpu.VMEM((16, 2, chans, cols), i16),
            pltpu.VMEM((16, 8, cols), f32),
            pltpu.VMEM((2, 16, chans, cols), i16),
            pltpu.VMEM((2, 16, chans, cols), i16),
            pltpu.VMEM((16, 4, chans, cols), f32),
            pltpu.VMEM((16, chans, cols), f32),
            pltpu.VMEM((16 * chans, cols), b16),
            pltpu.VMEM((2048, cols), b16),
            pltpu.VMEM((16 * chans, cols), f32),
            pltpu.VMEM((7, chans, cols), f32),
            dma((3,)), dma((3,)), dma((4,)), dma((4,)), dma((4, 4)), dma((4, 4)), dma((4, 4)), dma((4, 4)),
            dma((16,)), dma((16,)), dma((16,)), dma((16,)), dma((2,)), dma((2,)), dma((2, 16)), dma((2, 16)),
            dma((1,)),
        ],
        compiler_params=pltpu.CompilerParams(
            collective_id=0, has_side_effects=True, vmem_limit_bytes=60 * 1024 * 1024
        ),
    )(field, line(depth_dx), line(depth_dy), line(land_sea), cos_table, sin_table, own_table, own_w)
    result = (jnp.transpose(back, (1, 0, 2)).astype(jnp.float32) + HALF) * (TOP_E2 / LEVELS)
    return result.reshape(freqs, dirs, rows, cols)


def solution(mesh):
    placed = (
        P("freq", None, "space", None),
        P("space", None),
        P("freq"),
        P("freq"),
        P("space", None),
        P("space", None),
        P(None, "freq"),
        P("freq", None),
    )
    return jax.shard_map(
        body, mesh=mesh, in_specs=placed, out_specs=P("freq", None, "space", None), check_vma=False
    )
```

time: 453 us -> 154 us (0.34); the launches traced: 445 us -> 152 us
  blocking collectives: 236 us -> 0 us
  Pallas kernels: 0 us -> 127 us
  waiting for transfers between devices: 114 us -> 0.01 us
  other arithmetic: 25.3 us -> 4.04 us
  matrix products: 20.9 us -> 0 us
  between operations: 14 us -> 0.11 us
  starting transfers between devices: 13.5 us -> 6.42 us
  local copies, waits for them, and re-layouts: 21 us -> 14.1 us
    all_to_all x6 -> x0, blocking collectives: 236 us -> none  [the longest x2 108 us: body(): lax.all_to_all(scaled, 'freq', split_axis=2, concat_axis=0, tiled=True)]
    pallas_call x0 -> x1, Pallas kernels: none -> 127 us  [body(): pl.pallas_call(kernel, out_shape=jax.ShapeDtypeStruct((rows, chans, cols)...]
    all_gather x1 -> x0, waiting for transfers between devices: 110 us -> none  [rows_first(): out = lax.all_gather(both, axis, axis=0, tiled=True)]
    dot_general x2 -> x0, matrix products: 20.9 us -> none  [body(): lax.dot_general(out_whole, hidden, contract, preferred_element_type=jnp.f...]
    ppermute x4 -> x2, starting transfers between devices: 13.5 us -> 6.42 us  [the longest x1 4.5 us: body(): low = lax.ppermute(spectrum[:, :, rows - 1:], 'space', forward)]
    unnamed x20 -> x9, local copies, waits for them, and re-layouts: 7.54 us -> 1.2 us
    reduce_sum x4 -> x0, other arithmetic: 5.71 us -> none  [the longest x2 5.64 us: body(): partial_sum = jnp.sum(field, axis=(0, 1))]
    exp x2 -> x0, other arithmetic: 4.87 us -> none  [body(): field = field * jnp.exp(step_scale * jnp.tanh(returned.astype(jnp.float32)))]
  transfers between devices with their start and end apart: 5 -> 2, of which waited for: 2 -> 0; matrix products, arithmetic and copies ran while one was open for 3% -> 5% of each run, Pallas kernels for 0% -> 0%
where the time goes in v1:
time: 154 us; the launch traced here: 152 us
  Pallas kernels  127 us (82%)
  local copies, waits for them, and re-layouts  14.1 us (9%)
  starting transfers between devices  6.42 us (4%)
  other arithmetic  4.04 us (3%)
    pallas_call x1, Pallas kernels, body(): pl.pallas_call(kernel, out_shape=jax.ShapeDtypeStruct((rows, chans, cols)...  127 us
    ppermute x1, starting transfers between devices, body(): low = lax.ppermute(spectrum[:, :, rows - 1:], 'space', forward)  4.5 us
    reshape x3, local copies, waits for them, and re-layouts, line(): return a.astype(jnp.float32).reshape(rows, 1, cols)  3.41 us
  transfers between devices with their start and end apart: 2, of which 0 were waited for; matrix products, arithmetic and copies ran while one was open for 5% of the time, Pallas kernels for 0%

profile of v1, /device:TPU:1, one launch (start us, length us, event | category | flops | bytes accessed | tf_op | source)
XLA Modules:
  0.0 151.8 jit_solution(10313270651668668907)
XLA Ops:
  0.0 0.0 copy-start
  0.0 0.0 copy-start.2
  0.0 0.0 copy-start.1
  0.0 1.5 fusion.2
  1.5 4.5 %collective-permute-start = (f32[2,36,1,256]{3,1,2,0:T(8,128)S(1)}, f32[2,36,1,256]{3,1,2,0:T(8,128)S(1)}, u32[]{:S(2)}, u32[]{:S(2)}) collective-permute-start(f32[2,36,1,256]{3,1,2,0:T(8,128)S(1)} %copy.25), channel_id=1, source_target_pairs={{0,16},{16,32},{32,48},{48,64},{64,80},{80,96},{96,112},{112,128},... | collective-permute-start | bytes 221192 | tf_op jit(solution)/shard_map/ppermute | solution.py:445
  6.1 1.9 %collective-permute-start.1 = (f32[2,36,1,256]{3,1,2,0:T(8,128)S(1)}, f32[2,36,1,256]{3,1,2,0:T(8,128)S(1)}, u32[]{:S(2)}, u32[]{:S(2)}) collective-permute-start(f32[2,36,1,256]{3,1,2,0:T(8,128)S(1)} %copy.26), channel_id=1, source_target_pairs={{16,0},{32,16},{48,32},{64,48},{80,64},{96,80},{112,96},{128,112},... | collective-permute-start | bytes 221192 | tf_op jit(solution)/shard_map/ppermute | solution.py:446
  8.1 1.2 copy.21
  9.3 1.2 copy.22
  10.4 0.1 broadcast_in_dim.20
  10.5 0.1 broadcast_in_dim.22
  10.6 0.8 convert_element_type.7
  11.4 0.6 reshape.36.sea
  12.0 1.4 reshape.34.dx
  13.4 1.4 reshape.35.dy
  14.8 0.9 pad_maximum_fusion.1.own_w
  15.7 0.0 copy-done.2
  15.7 0.0 copy-done.1
  15.7 0.1 pad_maximum_fusion.2
  15.7 0.0 collective-permute-done
  15.7 0.1 copy.18
  15.8 0.0 collective-permute-done.1
  15.8 0.1 copy.19
  15.9 0.0 copy-done
  15.9 0.5 pad_maximum_fusion
  16.4 2.2 %copy.28 = f32[72,34,256]{2,0,1:T(8,128)} copy(f32[72,34,256]{2,1,0:T(8,128)S(1)} %bitcast.16) | data formatting | bytes 5013504 | tf_op jit(solution)/shard_map/reshape | solution.py:447
  18.7 0.7 broadcast_in_dim.21.cos_ref
  19.4 0.7 broadcast_in_dim.23.sin_ref
  20.1 0.7 broadcast_in_dim.24.own_table
  20.8 127.1 %shard_map.82 = s16[32,72,256]{2,1,0:T(8,128)(2,1)} custom-call(f32[34,72,256]{2,1,0:T(8,128)} %bitcast.17, f32[32,1,256]{2,1,0:T(1,128)} %reshape.34.dx, f32[32,1,256]{2,1,0:T(1,128)} %reshape.35.dy, f32[32,1,256]{2,1,0:T(1,128)} %reshape.36.sea, f32[72,256]{1,0:T(8,128)} %broadcast_in_dim.21.cos_ref, f32[72,256]{1,0:T(8,128)} %broadcast_in_dim.23.sin_ref, ...), custom_call_target="tpu_custom_call" | custom-call | tf_op jit(solution)/shard_map/pallas_call | solution.py:464
  147.9 1.7 %multiply_bitcast_fusion = f32[72,32,256]{2,0,1:T(8,128)S(1)} fusion(s16[32,72,256]{2,1,0:T(8,128)(2,1)} %shard_map.82), kind=kLoop, calls=%fused_computation.2 | loop fusion | flops 1769472 | bytes 3538944 | tf_op jit(solution)/shard_map/mul | solution.py:492
  149.6 2.1 %copy.23 = f32[72,32,256]{2,1,0:T(8,128)} copy(f32[72,32,256]{2,0,1:T(8,128)S(1)} %multiply_bitcast_fusion) | data formatting | bytes 4718592 | tf_op jit(solution)/shard_map/mul | solution.py:492
  (7 shorter events, 0.1 us)
Async XLA Ops:
  0.0 15.9 %copy-start = (f32[2,36,32,256]{3,2,1,0:T(8,128)S(1)}, f32[2,36,32,256]{3,2,1,0:T(8,128)}, u32[]{:S(2)}) copy-start(f32[2,36,32,256]{3,2,1,0:T(8,128)} %param.8) | copy-start | bytes 7077892
  0.0 15.7 %copy-start.2 = (f32[2]{0:T(128)S(1)}, f32[2]{0:T(128)}, u32[]{:S(2)}) copy-start(f32[2]{0:T(128)} %param.10) | copy-start | bytes 28
  0.0 15.7 %copy-start.1 = (f32[2]{0:T(128)S(1)}, f32[2]{0:T(128)}, u32[]{:S(2)}) copy-start(f32[2]{0:T(128)} %param.11) | copy-start | bytes 28
  1.5 14.2 %collective-permute-start = (f32[2,36,1,256]{3,1,2,0:T(8,128)S(1)}, f32[2,36,1,256]{3,1,2,0:T(8,128)S(1)}, u32[]{:S(2)}, u32[]{:S(2)}) collective-permute-start(f32[2,36,1,256]{3,1,2,0:T(8,128)S(1)} %copy.25), channel_id=1, source_target_pairs={{0,16},{16,32},{32,48},{48,64},{64,80},{80,96},{96,112},{112,128},... | collective-permute-start | bytes 221192 | tf_op jit(solution)/shard_map/ppermute | solution.py:445
  6.1 9.8 %collective-permute-start.1 = (f32[2,36,1,256]{3,1,2,0:T(8,128)S(1)}, f32[2,36,1,256]{3,1,2,0:T(8,128)S(1)}, u32[]{:S(2)}, u32[]{:S(2)}) collective-permute-start(f32[2,36,1,256]{3,1,2,0:T(8,128)S(1)} %copy.26), channel_id=1, source_target_pairs={{16,0},{32,16},{48,32},{64,48},{80,64},{96,80},{112,96},{128,112},... | collective-permute-start | bytes 221192 | tf_op jit(solution)/shard_map/ppermute | solution.py:446

commit v2 on v1

v2 whole, which is shorter than its diff:
```python
import math

import jax
import jax.numpy as jnp
import numpy as np
from jax import lax
from jax.experimental import pallas as pl
from jax.experimental.pallas import tpu as pltpu
from jax.sharding import PartitionSpec as P

DIRS = 36
MESH = pl.DeviceIdType.MESH

step_scale = 0.5
epsilon = 1e-06

TOP_T1 = 2.45
TOP_E1 = 4.06
TOP_E2 = 8.2
LEVELS = 65535.0
HALF = 32768.0


def encode(value, top):
    level = jnp.minimum(value * (LEVELS / top) + 0.5, LEVELS)
    return (level.astype(jnp.int32) - 32768).astype(jnp.int16)


def decode(code, top):
    return (code.astype(jnp.int32).astype(jnp.float32) + HALF) * (top / LEVELS)


def freq_of(rb, cb):
    high = rb // 4
    yy = rb % 4
    return (yy + high * (3 - 2 * yy)) * 4 + high * 2 + cb


def block_of(f):
    y = f // 4
    zl = f % 4
    high = zl // 2
    return high * 4 + y + high * (3 - 2 * y), zl % 2


def coefficients(table, cosine, sine):
    first = lax.broadcasted_iota(jnp.int32, cosine.shape, 0) < DIRS
    courant = jnp.where(first, table[0:1], table[1:2])
    refract = jnp.where(first, table[2:3], table[3:4])
    speed_x = courant * cosine
    speed_y = courant * sine
    pos_x = jnp.maximum(speed_x, 0.0)
    pos_y = jnp.maximum(speed_y, 0.0)
    keep = 1.0 - jnp.abs(speed_x) - jnp.abs(speed_y)
    return keep, pos_x, pos_x - speed_x, pos_y, pos_y - speed_y, refract * sine, refract * cosine


def transport_row(before, center, after, west_edge, east_edge, coef, dx, dy, sea):
    keep, pos_x, neg_x, pos_y, neg_y, turn_x, turn_y = coef
    rows, cols = center.shape
    lane = lax.broadcasted_iota(jnp.int32, center.shape, 1)
    west = jnp.where(lane == 0, west_edge, pltpu.roll(center, 1, 1))
    east = jnp.where(lane == cols - 1, east_edge, pltpu.roll(center, cols - 1, 1))
    shifted = center * keep + pos_x * before + neg_x * after + pos_y * west + neg_y * east
    turning = (turn_x * dx - turn_y * dy) * shifted
    moved_up = jnp.maximum(turning, 0.0)
    moved_down = jnp.maximum(-turning, 0.0)
    d = lax.broadcasted_iota(jnp.int32, center.shape, 0)
    lower = jnp.where((d == 0) | (d == DIRS), pltpu.roll(moved_up, DIRS + 1, 0), pltpu.roll(moved_up, 1, 0))
    upper = jnp.where(
        (d == DIRS - 1) | (d == rows - 1),
        pltpu.roll(moved_down, DIRS - 1, 0),
        pltpu.roll(moved_down, rows - 1, 0),
    )
    return (shifted - jnp.abs(turning) + lower + upper) * sea


def gelu(x):
    return 0.5 * x * (1.0 + jnp.tanh(math.sqrt(2.0 / math.pi) * (x + 0.044715 * x * x * x)))


def kernel(
    spectrum, dx, dy, land, courant, refract, cos_ref, sin_ref, w_in, w_out, out,
    field, own_table, own_w, weights, codes1, got1, codes2, got2, table, edge_out, edge_in, col_out, col_in,
    energy, moved, x_buf, h_buf, s_buf, coef_buf,
    z_send, z_recv, y_send, y_recv, x_send, x_recv, d_send, d_recv, a_send, a_recv, t_send, t_recv,
    e_send, e_recv, b_send, b_recv, halo_send, halo_recv, c_send, c_recv, local_sem,
):
    s = lax.axis_index("space")
    f = lax.axis_index("freq")
    core = s % 2
    x = (s // 2) % 4
    base = (s // 8) * 8
    y = f // 4
    zl = f % 4
    rb, cb = block_of(f)
    chans, rows, cols = spectrum.shape
    half = cols // 2
    groups = 16

    def at_freq(g):
        return {"space": s, "freq": g}

    def at_x(step):
        return {"space": base + ((x + step) % 4) * 2 + core, "freq": f}

    partner = {"space": s + 1 - 2 * core, "freq": f}
    above = {"space": jnp.maximum(s - 1, 0), "freq": f}
    below = {"space": jnp.minimum(s + 1, 15), "freq": f}
    has_up = jnp.logical_or(rb > 0, s > 0)
    has_down = jnp.logical_or(rb < 7, s < 15)
    up = {"space": jnp.where(rb > 0, s, jnp.maximum(s - 1, 0)), "freq": freq_of((rb + 7) % 8, cb)}
    down = {"space": jnp.where(rb < 7, s, jnp.minimum(s + 1, 15)), "freq": freq_of((rb + 1) % 8, cb)}
    beside = at_freq(freq_of(rb, 1 - cb))

    barrier = pltpu.get_barrier_semaphore()

    def greet(target):
        pl.semaphore_signal(barrier, inc=1, device_id=target, device_id_type=MESH)

    for k in range(1, groups):
        greet(at_freq((f + k) % 16))
    greet(at_x(1))
    greet(at_x(3))
    greet(partner)
    over_top = jnp.logical_and(rb == 0, s > 0)
    over_bottom = jnp.logical_and(rb == 7, s < 15)
    other_above = jnp.logical_and(core == 0, s > 0)
    other_below = jnp.logical_and(core == 1, s < 15)
    pl.when(over_top)(lambda: greet(up))
    pl.when(over_bottom)(lambda: greet(down))
    pl.when(other_above)(lambda: greet(above))
    pl.when(other_below)(lambda: greet(below))

    @pl.when(core == 0)
    def _():
        for k in range(9):
            own_w[k] = w_in[k].T

    @pl.when(core == 1)
    def _():
        for k in range(9):
            own_w[k] = w_out[:, k * 128 : (k + 1) * 128].T

    row_of = lax.broadcasted_iota(jnp.int32, (8, cols), 0)
    own_table[...] = jnp.where(
        row_of == 0, courant[0], jnp.where(row_of == 1, courant[1], jnp.where(row_of == 2, refract[0], refract[1]))
    )

    def turn(n):
        def some(c, carry):
            block = spectrum[pl.ds(c * 8, 8), pl.ds(n * 8, 8), :]
            field[pl.ds(n * 8 + 1, 8), pl.ds(pl.multiple_of(c * 8, 8), 8), :] = jnp.swapaxes(block, 0, 1)
            return carry

        lax.fori_loop(0, chans // 8, some, 0)

    turn(0)
    turn(3)
    known = (over_top, over_bottom, other_above, other_below)
    pl.semaphore_wait(barrier, 18 + sum(k.astype(jnp.int32) for k in known))

    def remote(src, dst, send, recv, target):
        return pltpu.make_async_remote_copy(
            src_ref=src, dst_ref=dst, send_sem=send, recv_sem=recv, device_id=target, device_id_type=MESH
        )

    def quarter(q):
        return pl.ds(pl.multiple_of(q * 32, 32), 32)

    own_quarter = weights.at[core, f, :, quarter(x), :]
    z_copies = []
    for k in range(1, 4):
        c = remote(
            own_w.at[:, quarter(x), :], own_quarter, z_send.at[k - 1], z_recv.at[k - 1], at_freq(y * 4 + (zl + k) % 4)
        )
        c.start()
        z_copies.append(c)
    to_above = remote(field.at[1], field.at[rows + 1], halo_send.at[0], halo_recv.at[1], above)
    to_below = remote(field.at[rows], field.at[0], halo_send.at[1], halo_recv.at[0], below)
    pl.when(s > 0)(to_above.start)
    pl.when(s < 15)(to_below.start)
    place = pltpu.make_async_copy(own_w.at[:, quarter(x), :], own_quarter, local_sem.at[0])
    place.start()
    table[f] = own_table[...]
    t_copies = []
    for k in range(1, groups):
        c = remote(own_table, table.at[f], t_send.at[k], t_recv.at[k], at_freq((f + k) % 16))
        c.start()
        t_copies.append(c)
    turn(1)
    turn(2)
    place.wait()

    def y_block(r, first=0, count=4, q=x):
        return weights.at[core, pl.ds(r * 4 + first, count), :, quarter(q), :]

    y_right, y_left = at_freq(((y + 1) % 4) * 4 + zl), at_freq(((y + 3) % 4) * 4 + zl)
    order = [y, (y + 3) % 4, (y + 1) % 4, (y + 2) % 4]
    xs = [x, (x + 3) % 4, (x + 1) % 4, (x + 2) % 4]
    y_copies, x_copies, d_copies = {}, {}, {}

    def go(where, key, copy):
        copy.start()
        where[key] = copy

    def spread(b):
        r = order[b]
        block = y_block(r)
        go(x_copies, (b, 0), remote(block, block, x_send.at[b, 0], x_recv.at[b, 0], at_x(1)))
        go(x_copies, (b, 1), remote(block, block, x_send.at[b, 1], x_recv.at[b, 1], at_x(3)))
        share(b, 0)

    def share(b, k):
        block = y_block(order[b], q=xs[k])
        go(d_copies, (b, k), remote(block, block, d_send.at[b, k], d_recv.at[b, k], partner))

    def weights_1():
        for c in z_copies:
            c.wait_recv()
        own = y_block(y)
        go(y_copies, 0, remote(own, own, y_send.at[0], y_recv.at[0], y_right))
        go(y_copies, 1, remote(own, own, y_send.at[1], y_recv.at[1], y_left))
        spread(0)

    def weights_2():
        y_copies[0].wait_recv()
        part = y_block(order[1], 0, 2)
        go(y_copies, 2, remote(part, part, y_send.at[2], y_recv.at[2], y_right))
        spread(1)

    def weights_3():
        y_copies[1].wait_recv()
        part = y_block(order[2], 2, 2)
        go(y_copies, 3, remote(part, part, y_send.at[3], y_recv.at[3], y_left))
        spread(2)

    def weights_4():
        y_copies[2].wait_recv()
        y_copies[3].wait_recv()
        spread(3)

    def weights_5(b):
        x_copies[b, 0].wait_recv()
        part = y_block(order[b], 0, 2, xs[1])
        go(x_copies, (b, 2), remote(part, part, x_send.at[b, 2], x_recv.at[b, 2], at_x(1)))
        share(b, 1)
        x_copies[b, 1].wait_recv()
        part = y_block(order[b], 2, 2, xs[2])
        go(x_copies, (b, 3), remote(part, part, x_send.at[b, 3], x_recv.at[b, 3], at_x(3)))
        share(b, 2)

    def weights_6(b):
        x_copies[b, 2].wait_recv()
        x_copies[b, 3].wait_recv()
        share(b, 3)

    coef = coefficients(own_table[...], cos_ref[...], sin_ref[...])
    for i, c in enumerate(coef):
        coef_buf[i] = c

    @pl.when(s > 0)
    def _():
        to_below.wait_recv()

    @pl.when(s == 0)
    def _():
        field[0] = jnp.zeros((chans, cols), jnp.float32)

    @pl.when(s < 15)
    def _():
        to_above.wait_recv()

    @pl.when(s == 15)
    def _():
        field[rows + 1] = jnp.zeros((chans, cols), jnp.float32)

    def first_rows(n):
        def one(r, carry):
            row = n * 4 + r
            value = transport_row(
                field[row], field[row + 1], field[row + 2], 0.0, 0.0, [coef_buf[i] for i in range(7)],
                dx[pl.ds(row, 1), :], dy[pl.ds(row, 1), :], land[pl.ds(row, 1), :].astype(jnp.float32),
            )
            code = encode(value, TOP_T1)
            codes1[n * 2, r] = code[:, :half]
            codes1[n * 2 + 1, r] = code[:, half:]
            return carry

        lax.fori_loop(0, 4, one, 0)

    def first_copy(k, c):
        n = (rb + k) % 8
        return remote(codes1.at[n * 2 + c], got1.at[f], a_send.at[k, c], a_recv.at[k, cb], at_freq(freq_of(n, c)))

    def first_and_send(k, carry):
        first_rows((rb + k) % 8)
        first_copy(k, 0).start()
        first_copy(k, 1).start()
        return carry

    lax.fori_loop(1, 8, first_and_send, 0)
    first_rows(rb)
    first_copy(0, 1 - cb).start()
    mine = pltpu.make_async_copy(codes1.at[rb * 2 + cb], got1.at[f], local_sem.at[0])
    mine.start()
    weights_1()
    weights_2()
    weights_3()
    weights_4()
    mine.wait()
    for b in range(4):
        weights_5(b)

    def first_arrival(k, c):
        g = freq_of((rb + 8 - k) % 8, c)
        return remote(codes1.at[0], got1.at[g], a_send.at[k, 0], a_recv.at[k, c], at_freq(g))

    def await_rows(k, carry):
        first_arrival(k, 0).wait_recv()
        first_arrival(k, 1).wait_recv()
        return carry

    lax.fori_loop(1, 8, await_rows, 0)
    first_arrival(0, 1 - cb).wait_recv()
    for b in range(4):
        weights_6(b)
    for c in d_copies.values():
        c.wait_recv()

    def network():
        def first_layer(i, carry):
            lhs = jnp.concatenate(
                [
                    jnp.concatenate([weights[0, i * 4 + q, k] for k in range(9)], axis=1)
                    for q in range(4)
                ],
                axis=0,
            )
            pre = jnp.dot(lhs, x_buf[...], preferred_element_type=jnp.float32)
            h_buf[pl.ds(pl.multiple_of(i * 512, 512), 512), :] = gelu(pre).astype(jnp.bfloat16)
            return carry

        lax.fori_loop(0, 4, first_layer, 0)

        def second_layer(i, carry):
            lhs = jnp.concatenate(
                [
                    jnp.concatenate([weights[1, g, i * 3 + k] for g in range(16)], axis=1)
                    for k in range(3)
                ],
                axis=0,
            )
            s_buf[pl.ds(pl.multiple_of(i * 384, 384), 384), :] = jnp.dot(
                lhs, h_buf[...], preferred_element_type=jnp.float32
            )
            return carry

        lax.fori_loop(0, 3, second_layer, 0)

    def scale_into_x(total):
        mean = jnp.sum(total, axis=0, keepdims=True) * (1.0 / 1152.0) + epsilon
        inverse = 1.0 / mean

        def pair(p, carry):
            both = jnp.concatenate([moved[p * 2], moved[p * 2 + 1]], axis=0) * inverse
            x_buf[pl.ds(pl.multiple_of(p * 144, 144), 144), :] = both.astype(jnp.bfloat16)
            return carry

        lax.fori_loop(0, 8, pair, 0)

    def growth(g):
        return jnp.exp(step_scale * jnp.tanh(s_buf[pl.ds(pl.multiple_of(g * 72, 8), 72), :]))

    zeros = jnp.zeros((chans, cols), jnp.float32)
    thin = zeros[:, :half]
    lane = lax.broadcasted_iota(jnp.int32, (chans, half), 1)

    edge_copies = [
        remote(edge_out.at[0], edge_in.at[1], e_send.at[0], e_recv.at[1], up),
        remote(edge_out.at[1], edge_in.at[0], e_send.at[1], e_recv.at[0], down),
    ]
    for first, last in ((0, 3), (1, 2)):

        def load(g, total):
            value = decode(jnp.concatenate([got1[g, first], got1[g, last]], axis=1), TOP_T1)
            moved[g] = value
            return total + value

        scale_into_x(lax.fori_loop(0, groups, load, zeros))
        network()

        def update(g, carry):
            value = moved[g] * growth(g)
            energy[g, first + 1] = value[:, :half]
            energy[g, last + 1] = value[:, half:]
            if first == 0:
                code = encode(value, TOP_E1)
                edge_out[0, g] = code[:, :half]
                edge_out[1, g] = code[:, half:]
            return carry

        lax.fori_loop(0, groups, update, 0)
        if first == 0:
            pl.when(has_up)(edge_copies[0].start)
            pl.when(has_down)(edge_copies[1].start)

    edge_lane = (half - 1) * (1 - cb)

    def pack(g, block):
        for r in range(4):
            at = g * 4 + r
            turned = pltpu.roll(energy[g, r + 1], (at - edge_lane + half) % half, 1)
            block = jnp.where(lane == at, turned, block)
        return block

    col_out[...] = lax.fori_loop(0, groups, pack, thin)
    col_copy = remote(col_out, col_in, c_send.at[0], c_recv.at[0], beside)
    col_copy.start()
    for k in range(1, groups):
        t_copies[k - 1].wait_recv()
    west_side = cb.astype(jnp.float32)
    land_lane = (half - 1) * (1 - cb)

    def my_half(line):
        return jnp.where(cb == 0, line[:, :half], line[:, half:])

    col_copy.wait_recv()

    def fill(present, copy, slot, row):
        @pl.when(present)
        def _():
            copy.wait_recv()

            def some(g, carry):
                energy[g, row] = decode(edge_in[slot, g], TOP_E1)
                return carry

            lax.fori_loop(0, groups, some, 0)

        @pl.when(jnp.logical_not(present))
        def _():
            def some(g, carry):
                energy[g, row] = thin
                return carry

            lax.fori_loop(0, groups, some, 0)

    for n, pair in enumerate(((1, 2), (0, 3))):
        if n == 1:
            fill(has_up, edge_copies[1], 0, 0)
            fill(has_down, edge_copies[0], 1, 5)

        def second(g, total):
            coef = coefficients(table[g][:, :half], cos_ref[:, :half], sin_ref[:, :half])
            done = []
            for r in pair:
                row = pl.ds(rb * 4 + r, 1)
                side = pltpu.roll(col_in[...], (land_lane - (g * 4 + r) + half) % half, 1)
                done.append(
                    transport_row(
                        energy[g, r], energy[g, r + 1], energy[g, r + 2], side * west_side, side * (1.0 - west_side),
                        coef, my_half(dx[row, :]), my_half(dy[row, :]), my_half(land[row, :]).astype(jnp.float32),
                    )
                )
            value = jnp.concatenate(done, axis=1)
            moved[g] = value
            return total + value

        scale_into_x(lax.fori_loop(0, groups, second, zeros))
        network()

        def finish(k):
            g = (f + k) % 16
            code = encode(moved[g] * growth(g), TOP_E2)
            codes2[g, n * 2] = code[:, :half]
            codes2[g, n * 2 + 1] = code[:, half:]

        def finish_and_send(k, carry):
            finish(k)
            g = (f + k) % 16
            two = pl.ds(n * 2, 2)
            remote(codes2.at[g, two], got2.at[rb * 2 + cb, two], b_send.at[n, k], b_recv.at[n, k], at_freq(g)).start()
            return carry

        lax.fori_loop(1, groups, finish_and_send, 0)
        finish(0)

    own_back = pltpu.make_async_copy(codes2.at[f], got2.at[rb * 2 + cb], local_sem.at[0])
    own_back.start()

    def await_back(k, carry):
        g = (f + 16 - k) % 16
        b, c = block_of(g)
        for n in range(2):
            two = pl.ds(n * 2, 2)
            remote(codes2.at[0, two], got2.at[b * 2 + c, two], b_send.at[n, k], b_recv.at[n, k], at_freq(g)).wait_recv()
        return carry

    lax.fori_loop(1, groups, await_back, 0)
    own_back.wait()

    def put(j, carry):
        out[j] = got2[j]
        return carry

    lax.fori_loop(0, groups, put, 0)

    for c in z_copies + t_copies + list(y_copies.values()) + list(x_copies.values()) + list(d_copies.values()):
        c.wait_send()

    def sent(k, carry):
        for n in range(2):
            two = pl.ds(n * 2, 2)
            remote(codes2.at[0, two], got2.at[0, two], b_send.at[n, k], b_recv.at[n, k], partner).wait_send()
        return carry

    lax.fori_loop(1, groups, sent, 0)

    def sent_first(k, carry):
        first_copy(k, 0).wait_send()
        first_copy(k, 1).wait_send()
        return carry

    lax.fori_loop(1, 8, sent_first, 0)
    first_copy(0, 1 - cb).wait_send()
    col_copy.wait_send()
    pl.when(s > 0)(to_above.wait_send)
    pl.when(s < 15)(to_below.wait_send)
    pl.when(has_up)(edge_copies[0].wait_send)
    pl.when(has_down)(edge_copies[1].wait_send)


def turn_back(codes, out):
    chans = out.shape[0]
    half = codes.shape[-1]
    slot = (2, 0, 1, 3)

    def some(c, carry):
        part = pl.ds(pl.multiple_of(c * 8, 8), 8)
        for side in range(2):
            lines = [decode(codes[n, side, slot[r], part, :], TOP_E2)[None] for n in range(2) for r in range(4)]
            out[part, :, side * half : (side + 1) * half] = jnp.swapaxes(jnp.concatenate(lines, axis=0), 0, 1)
        return carry

    lax.fori_loop(0, chans // 8, some, 0)


def body(spectrum, land_sea, courant, refract, depth_dx, depth_dy, w_in, w_out):
    freqs, dirs, rows, cols = spectrum.shape
    chans = freqs * dirs
    half = cols // 2
    angles = (np.arange(DIRS, dtype=np.float32) + np.float32(0.5)) * np.float32(2.0 * math.pi / DIRS)
    cos_table = np.ascontiguousarray(np.broadcast_to(np.tile(np.cos(angles), freqs)[:, None], (chans, cols)))
    sin_table = np.ascontiguousarray(np.broadcast_to(np.tile(np.sin(angles), freqs)[:, None], (chans, cols)))
    vmem = pl.BlockSpec(memory_space=pltpu.VMEM)
    smem = pl.BlockSpec(memory_space=pltpu.SMEM)
    dma = pltpu.SemaphoreType.DMA
    i16, f32, b16 = jnp.int16, jnp.float32, jnp.bfloat16
    back = pl.pallas_call(
        kernel,
        out_shape=jax.ShapeDtypeStruct((16, 4, chans, half), i16),
        in_specs=[vmem] * 4 + [smem] * 2 + [vmem] * 4,
        out_specs=vmem,
        scratch_shapes=[
            pltpu.VMEM((rows + 2, chans, cols), f32),
            pltpu.VMEM((8, cols), f32),
            pltpu.VMEM((9, 128, 128), b16),
            pltpu.VMEM((2, 16, 9, 128, 128), b16),
            pltpu.VMEM((16, 4, chans, half), i16),
            pltpu.VMEM((16, 4, chans, half), i16),
            pltpu.VMEM((16, 4, chans, half), i16),
            pltpu.VMEM((16, 4, chans, half), i16),
            pltpu.VMEM((16, 8, cols), f32),
            pltpu.VMEM((2, 16, chans, half), i16),
            pltpu.VMEM((2, 16, chans, half), i16),
            pltpu.VMEM((chans, half), f32),
            pltpu.VMEM((chans, half), f32),
            pltpu.VMEM((16, 6, chans, half), f32),
            pltpu.VMEM((16, chans, cols), f32),
            pltpu.VMEM((16 * chans, cols), b16),
            pltpu.VMEM((2048, cols), b16),
            pltpu.VMEM((16 * chans, cols), f32),
            pltpu.VMEM((7, chans, cols), f32),
            dma((3,)), dma((3,)), dma((4,)), dma((4,)), dma((4, 4)), dma((4, 4)), dma((4, 4)), dma((4, 4)),
            dma((8, 2)), dma((8, 2)), dma((16,)), dma((16,)), dma((2,)), dma((2,)), dma((2, 16)), dma((2, 16)),
            dma((2,)), dma((2,)), dma((1,)), dma((1,)), dma((1,)),
        ],
        compiler_params=pltpu.CompilerParams(
            collective_id=0, has_side_effects=True, vmem_limit_bytes=60 * 1024 * 1024
        ),
    )(
        spectrum.reshape(chans, rows, cols), depth_dx, depth_dy, land_sea, courant, refract, cos_table, sin_table,
        w_in.reshape(9, 128, 128), w_out,
    )
    result = pl.pallas_call(
        turn_back,
        grid=(4,),
        out_shape=jax.ShapeDtypeStruct((chans, rows, cols), f32),
        in_specs=[pl.BlockSpec((2, 2, 4, chans, half), lambda i: (i, 0, 0, 0, 0))],
        out_specs=pl.BlockSpec((chans, 8, cols), lambda i: (0, i, 0)),
    )(back.reshape(8, 2, 4, chans, half))
    return result.reshape(freqs, dirs, rows, cols)


def solution(mesh):
    placed = (
        P("freq", None, "space", None),
        P("space", None),
        P("freq"),
        P("freq"),
        P("space", None),
        P("space", None),
        P(None, "freq"),
        P("freq", None),
    )
    return jax.shard_map(
        body, mesh=mesh, in_specs=placed, out_specs=P("freq", None, "space", None), check_vma=False
    )
```

time: 154 us -> 126 us (0.82)
  the two profiles are of different devices: /device:TPU:1 before, /device:TPU:248 now
where the time goes in v2:
time: 126 us
  Pallas kernels  126 us (100%)
    pallas_call x1, Pallas kernels, body(): pl.pallas_call(kernel, out_shape=jax.ShapeDtypeStruct((16, 4, chans, half...  122 us
    pallas_call x1, Pallas kernels, body(): pl.pallas_call(turn_back, grid=(4,), out_shape=jax.ShapeDtypeStruct((chan...  4.04 us

profile of v2, /device:TPU:248, one launch (start us, length us, event | category | flops | bytes accessed | tf_op | source)
XLA Modules:
  0.0 125.6 jit_solution(8742766936836607105)
XLA Ops:
  0.0 121.5 %shard_map.100 = s16[16,4,72,128]{3,2,1,0:T(8,128)(2,1)} custom-call(f32[72,32,256]{2,1,0:T(8,128)} %bitcast.5, f32[32,256]{1,0:T(8,128)} %dx.1, f32[32,256]{1,0:T(8,128)} %dy.1, s32[32,256]{1,0:T(8,128)} %land.1, f32[2]{0:T(128)} %courant.1, f32[2]{0:T(128)} %refract.1, f32[72,256]{1,0:T(8,128)} %constant.4.clone.cos_ref, f32[72,256]{1,0:T(8,128)} %constant.5.clone.sin_ref, ...), custom_call_target="tpu_custom_call" | custom-call | tf_op jit(solution)/shard_map/pallas_call | solution.py:560
  121.5 4.0 %shard_map.101 = f32[72,32,256]{2,1,0:T(8,128)} custom-call(s16[8,2,4,72,128]{4,3,2,1,0:T(8,128)(2,1)} %bitcast.4), custom_call_target="tpu_custom_call" | custom-call | tf_op jit(solution)/shard_map/pallas_call | solution.py:596

commit v3 on v2

--- a/solution.py
+++ b/solution.py
@@ -80,11 +80,13 @@
 
 
 def kernel(
-    spectrum, dx, dy, land, courant, refract, cos_ref, sin_ref, w_in, w_out, out,
+    spectrum_in, dx_in, dy_in, land_in, courant, refract, cos_in, sin_in, w_in_in, w_out_in, out,
+    spectrum, dx, dy, land, cos_ref, sin_ref, w_in, w_out,
     field, own_table, own_w, weights, codes1, got1, codes2, got2, table, edge_out, edge_in, col_out, col_in,
     energy, moved, x_buf, h_buf, s_buf, coef_buf,
     z_send, z_recv, y_send, y_recv, x_send, x_recv, d_send, d_recv, a_send, a_recv, t_send, t_recv,
-    e_send, e_recv, b_send, b_recv, halo_send, halo_recv, c_send, c_recv, local_sem,
+    e_send, e_recv, b_send, b_recv, halo_send, halo_recv, c_send, c_recv, l_send, l_recv, m_send, m_recv,
+    local_sem, load_sem, store_sem,
 ):
     s = lax.axis_index("space")
     f = lax.axis_index("freq")
@@ -132,6 +134,20 @@
     pl.when(other_above)(lambda: greet(above))
     pl.when(other_below)(lambda: greet(below))
 
+    loads = [
+        pltpu.make_async_copy(src, dst, load_sem.at[i])
+        for i, (src, dst) in enumerate(
+            (
+                (w_in_in, w_in), (w_out_in, w_out), (spectrum_in, spectrum), (cos_in, cos_ref), (sin_in, sin_ref),
+                (dx_in, dx), (dy_in, dy), (land_in, land),
+            )
+        )
+    ]
+    for c in loads:
+        c.start()
+    loads[0].wait()
+    loads[1].wait()
+
     @pl.when(core == 0)
     def _():
         for k in range(9):
@@ -155,6 +171,7 @@
 
         lax.fori_loop(0, chans // 8, some, 0)
 
+    loads[2].wait()
     turn(0)
     turn(3)
     known = (over_top, over_bottom, other_above, other_below)
@@ -190,70 +207,95 @@
         t_copies.append(c)
     turn(1)
     turn(2)
+    for c in loads[3:]:
+        c.wait()
     place.wait()
-
-    def y_block(r, first=0, count=4, q=x):
-        return weights.at[core, pl.ds(r * 4 + first, count), :, quarter(q), :]
 
     y_right, y_left = at_freq(((y + 1) % 4) * 4 + zl), at_freq(((y + 3) % 4) * 4 + zl)
     order = [y, (y + 3) % 4, (y + 1) % 4, (y + 2) % 4]
     xs = [x, (x + 3) % 4, (x + 1) % 4, (x + 2) % 4]
-    y_copies, x_copies, d_copies = {}, {}, {}
-
-    def go(where, key, copy):
-        copy.start()
-        where[key] = copy
+    whole, front, rear = (0, 9), (0, 5), (5, 4)
+    copies = {}
+
+    def by_quarter(b, q, ks=whole, count=None):
+        count = (4 if b == 0 else 3) if count is None else count
+        return weights.at[core, pl.ds(order[b] * 4, count), pl.ds(*ks), quarter(q), :]
+
+    def by_piece(b, ks=whole):
+        return weights.at[core, order[b] * 4 + 3, pl.ds(*ks)]
+
+    def go(key, block, send, recv, target):
+        c = remote(block, block, send, recv, target)
+        c.start()
+        copies[key] = c
+
+    def got(*key):
+        copies[key].wait_recv()
 
     def spread(b):
-        r = order[b]
-        block = y_block(r)
-        go(x_copies, (b, 0), remote(block, block, x_send.at[b, 0], x_recv.at[b, 0], at_x(1)))
-        go(x_copies, (b, 1), remote(block, block, x_send.at[b, 1], x_recv.at[b, 1], at_x(3)))
+        block = by_quarter(b, x)
+        go(("x", b, 0), block, x_send.at[b, 0], x_recv.at[b, 0], at_x(1))
+        go(("x", b, 1), block, x_send.at[b, 1], x_recv.at[b, 1], at_x(3))
         share(b, 0)
 
     def share(b, k):
-        block = y_block(order[b], q=xs[k])
-        go(d_copies, (b, k), remote(block, block, d_send.at[b, k], d_recv.at[b, k], partner))
+        go(("d", b, k), by_quarter(b, xs[k]), d_send.at[b, k], d_recv.at[b, k], partner)
+
+    def share_piece(b):
+        go(("m", b), by_piece(b), m_send.at[b], m_recv.at[b], partner)
 
     def weights_1():
         for c in z_copies:
             c.wait_recv()
-        own = y_block(y)
-        go(y_copies, 0, remote(own, own, y_send.at[0], y_recv.at[0], y_right))
-        go(y_copies, 1, remote(own, own, y_send.at[1], y_recv.at[1], y_left))
+        own = by_quarter(0, x, count=3)
+        go(("y", 0), own, y_send.at[0], y_recv.at[0], y_right)
+        go(("y", 1), own, y_send.at[1], y_recv.at[1], y_left)
         spread(0)
 
     def weights_2():
-        y_copies[0].wait_recv()
-        part = y_block(order[1], 0, 2)
-        go(y_copies, 2, remote(part, part, y_send.at[2], y_recv.at[2], y_right))
+        got("y", 0)
+        go(("y", 2), by_quarter(1, x, front), y_send.at[2], y_recv.at[2], y_right)
         spread(1)
 
     def weights_3():
-        y_copies[1].wait_recv()
-        part = y_block(order[2], 2, 2)
-        go(y_copies, 3, remote(part, part, y_send.at[3], y_recv.at[3], y_left))
+        got("y", 1)
+        go(("y", 3), by_quarter(2, x, rear), y_send.at[3], y_recv.at[3], y_left)
         spread(2)
 
     def weights_4():
-        y_copies[2].wait_recv()
-        y_copies[3].wait_recv()
+        got("y", 2)
+        got("y", 3)
         spread(3)
 
     def weights_5(b):
-        x_copies[b, 0].wait_recv()
-        part = y_block(order[b], 0, 2, xs[1])
-        go(x_copies, (b, 2), remote(part, part, x_send.at[b, 2], x_recv.at[b, 2], at_x(1)))
+        got("x", b, 0)
+        go(("x", b, 2), by_quarter(b, xs[1], front), x_send.at[b, 2], x_recv.at[b, 2], at_x(1))
         share(b, 1)
-        x_copies[b, 1].wait_recv()
-        part = y_block(order[b], 2, 2, xs[2])
-        go(x_copies, (b, 3), remote(part, part, x_send.at[b, 3], x_recv.at[b, 3], at_x(3)))
+        got("x", b, 1)
+        go(("x", b, 3), by_quarter(b, xs[2], rear), x_send.at[b, 3], x_recv.at[b, 3], at_x(3))
         share(b, 2)
 
     def weights_6(b):
-        x_copies[b, 2].wait_recv()
-        x_copies[b, 3].wait_recv()
+        got("x", b, 2)
+        got("x", b, 3)
         share(b, 3)
+
+    def pieces_1():
+        go(("l", 0), by_piece(0), l_send.at[0], l_recv.at[0], y_right)
+        go(("l", 1), by_piece(0), l_send.at[1], l_recv.at[1], y_left)
+
+    def pieces_2():
+        got("l", 0)
+        go(("l", 2), by_piece(1, front), l_send.at[2], l_recv.at[2], y_right)
+        share_piece(1)
+        got("l", 1)
+        go(("l", 3), by_piece(2, rear), l_send.at[3], l_recv.at[3], y_left)
+        share_piece(2)
+
+    def pieces_3():
+        got("l", 2)
+        got("l", 3)
+        share_piece(3)
 
     coef = coefficients(own_table[...], cos_ref[...], sin_ref[...])
     for i, c in enumerate(coef):
@@ -289,61 +331,66 @@
 
         lax.fori_loop(0, 4, one, 0)
 
-    def first_copy(k, c):
-        n = (rb + k) % 8
-        return remote(codes1.at[n * 2 + c], got1.at[f], a_send.at[k, c], a_recv.at[k, cb], at_freq(freq_of(n, c)))
-
-    def first_and_send(k, carry):
-        first_rows((rb + k) % 8)
-        first_copy(k, 0).start()
-        first_copy(k, 1).start()
+    def first_copy(i):
+        ky, kz = i // 4, i % 4
+        g = ((y + ky) % 4) * 4 + (zl + kz) % 4
+        n, c = block_of(g)
+        return remote(codes1.at[n * 2 + c], got1.at[f], a_send.at[i], a_recv.at[i], at_freq(g))
+
+    def first_send(i, carry):
+        first_copy(i).start()
         return carry
 
-    lax.fori_loop(1, 8, first_and_send, 0)
-    first_rows(rb)
-    first_copy(0, 1 - cb).start()
+    def first_arrival(i, carry):
+        g = ((y + 4 - i // 4) % 4) * 4 + (zl + 4 - i % 4) % 4
+        remote(codes1.at[0], got1.at[g], a_send.at[i], a_recv.at[i], at_freq(g)).wait_recv()
+        return carry
+
+    def all_rows(n, carry):
+        first_rows(n)
+        return carry
+
+    lax.fori_loop(0, 8, all_rows, 0)
     mine = pltpu.make_async_copy(codes1.at[rb * 2 + cb], got1.at[f], local_sem.at[0])
     mine.start()
     weights_1()
+    lax.fori_loop(1, 4, first_send, 0)
     weights_2()
+    weights_5(0)
     weights_3()
+    lax.fori_loop(4, 16, first_send, 0)
+    mine.wait()
     weights_4()
-    mine.wait()
-    for b in range(4):
-        weights_5(b)
-
-    def first_arrival(k, c):
-        g = freq_of((rb + 8 - k) % 8, c)
-        return remote(codes1.at[0], got1.at[g], a_send.at[k, 0], a_recv.at[k, c], at_freq(g))
-
-    def await_rows(k, carry):
-        first_arrival(k, 0).wait_recv()
-        first_arrival(k, 1).wait_recv()
-        return carry
-
-    lax.fori_loop(1, 8, await_rows, 0)
-    first_arrival(0, 1 - cb).wait_recv()
-    for b in range(4):
-        weights_6(b)
-    for c in d_copies.values():
-        c.wait_recv()
-
-    def network():
-        def first_layer(i, carry):
-            lhs = jnp.concatenate(
-                [
-                    jnp.concatenate([weights[0, i * 4 + q, k] for k in range(9)], axis=1)
-                    for q in range(4)
-                ],
-                axis=0,
-            )
-            pre = jnp.dot(lhs, x_buf[...], preferred_element_type=jnp.float32)
-            h_buf[pl.ds(pl.multiple_of(i * 512, 512), 512), :] = gelu(pre).astype(jnp.bfloat16)
-            return carry
-
-        lax.fori_loop(0, 4, first_layer, 0)
-
-        def second_layer(i, carry):
+    weights_6(0)
+    pieces_1()
+    weights_5(1)
+    weights_5(2)
+    pieces_2()
+
+    def rows_of(hidden, blocks, size):
+        for n, at in enumerate(blocks):
+            yield pl.ds(pl.multiple_of(at, size), size), hidden[n * size : (n + 1) * size]
+
+    def first_quarter(q, p):
+        pieces = [b * 4 + n for b in range(4) for n in range(3)]
+        lhs = jnp.concatenate(
+            [jnp.concatenate([weights[0, g, k, quarter(q), :] for k in range(9)], axis=1) for g in pieces], axis=0
+        )
+        hidden = gelu(jnp.dot(lhs, x_buf[p], preferred_element_type=jnp.float32)).astype(jnp.bfloat16)
+        for where, part in rows_of(hidden, [g * 128 + q * 32 for g in pieces], 32):
+            h_buf[p, where, :] = part
+
+    def first_rest(p):
+        pieces = [b * 4 + 3 for b in range(4)]
+        lhs = jnp.concatenate(
+            [jnp.concatenate([weights[0, g, k] for k in range(9)], axis=1) for g in pieces], axis=0
+        )
+        hidden = gelu(jnp.dot(lhs, x_buf[p], preferred_element_type=jnp.float32)).astype(jnp.bfloat16)
+        for where, part in rows_of(hidden, [g * 128 for g in pieces], 128):
+            h_buf[p, where, :] = part
+
+    def second_layer(p):
+        def some(i, carry):
             lhs = jnp.concatenate(
                 [
                     jnp.concatenate([weights[1, g, i * 3 + k] for g in range(16)], axis=1)
@@ -352,19 +399,19 @@
                 axis=0,
             )
             s_buf[pl.ds(pl.multiple_of(i * 384, 384), 384), :] = jnp.dot(
-                lhs, h_buf[...], preferred_element_type=jnp.float32
+                lhs, h_buf[p], preferred_element_type=jnp.float32
             )
             return carry
 
-        lax.fori_loop(0, 3, second_layer, 0)
-
-    def scale_into_x(total):
+        lax.fori_loop(0, 3, some, 0)
+
+    def scale_into_x(total, p):
         mean = jnp.sum(total, axis=0, keepdims=True) * (1.0 / 1152.0) + epsilon
         inverse = 1.0 / mean
 
-        def pair(p, carry):
-            both = jnp.concatenate([moved[p * 2], moved[p * 2 + 1]], axis=0) * inverse
-            x_buf[pl.ds(pl.multiple_of(p * 144, 144), 144), :] = both.astype(jnp.bfloat16)
+        def pair(n, carry):
+            both = jnp.concatenate([moved[n * 2], moved[n * 2 + 1]], axis=0) * inverse
+            x_buf[p, pl.ds(pl.multiple_of(n * 144, 144), 144), :] = both.astype(jnp.bfloat16)
             return carry
 
         lax.fori_loop(0, 8, pair, 0)
@@ -380,18 +427,53 @@
         remote(edge_out.at[0], edge_in.at[1], e_send.at[0], e_recv.at[1], up),
         remote(edge_out.at[1], edge_in.at[0], e_send.at[1], e_recv.at[0], down),
     ]
-    for first, last in ((0, 3), (1, 2)):
+    lax.fori_loop(1, 16, first_arrival, 0)
+    pairs = ((0, 3), (1, 2))
+
+    def both_of(g, pair):
+        return decode(jnp.concatenate([got1[g, pair[0]], got1[g, pair[1]]], axis=1), TOP_T1)
+
+    for p in range(2):
 
         def load(g, total):
-            value = decode(jnp.concatenate([got1[g, first], got1[g, last]], axis=1), TOP_T1)
+            value = both_of(g, pairs[p])
             moved[g] = value
             return total + value
 
-        scale_into_x(lax.fori_loop(0, groups, load, zeros))
-        network()
+        scale_into_x(lax.fori_loop(0, groups, load, zeros), p)
+
+    def first_layer_of(i):
+        for b in range(4):
+            got("d", b, i)
+
+        def one(p, carry):
+            first_quarter(xs[i], p)
+            return carry
+
+        lax.fori_loop(0, 2, one, 0)
+
+    first_layer_of(0)
+    weights_5(3)
+    pieces_3()
+    first_layer_of(1)
+    weights_6(1)
+    first_layer_of(2)
+    weights_6(2)
+    weights_6(3)
+    first_layer_of(3)
+    for b in range(1, 4):
+        got("m", b)
+
+    def last_one(p, carry):
+        first_rest(p)
+        return carry
+
+    lax.fori_loop(0, 2, last_one, 0)
+    for p, (first, last) in enumerate(pairs):
+        second_layer(p)
 
         def update(g, carry):
-            value = moved[g] * growth(g)
+            value = both_of(g, pairs[p]) * growth(g)
             energy[g, first + 1] = value[:, :half]
             energy[g, last + 1] = value[:, half:]
             if first == 0:
@@ -414,7 +496,7 @@
             block = jnp.where(lane == at, turned, block)
         return block
 
-    col_out[...] = lax.fori_loop(0, groups, pack, thin)
+    col_out[...] = lax.fori_loop(0, groups, pack, thin, unroll=4)
     col_copy = remote(col_out, col_in, c_send.at[0], c_recv.at[0], beside)
     col_copy.start()
     for k in range(1, groups):
@@ -467,8 +549,15 @@
             moved[g] = value
             return total + value
 
-        scale_into_x(lax.fori_loop(0, groups, second, zeros))
-        network()
+        scale_into_x(lax.fori_loop(0, groups, second, zeros), n)
+
+        def quarters(q, carry):
+            first_quarter(q, n)
+            return carry
+
+        lax.fori_loop(0, 4, quarters, 0)
+        first_rest(n)
+        second_layer(n)
 
         def finish(k):
             g = (f + k) % 16
@@ -495,18 +584,17 @@
         for n in range(2):
             two = pl.ds(n * 2, 2)
             remote(codes2.at[0, two], got2.at[b * 2 + c, two], b_send.at[n, k], b_recv.at[n, k], at_freq(g)).wait_recv()
+        put(b * 2 + c).start()
         return carry
 
+    def put(n):
+        return pltpu.make_async_copy(got2.at[n], out.at[n], store_sem.at[n])
+
+    own_back.wait()
+    put(rb * 2 + cb).start()
     lax.fori_loop(1, groups, await_back, 0)
-    own_back.wait()
-
-    def put(j, carry):
-        out[j] = got2[j]
-        return carry
-
-    lax.fori_loop(0, groups, put, 0)
-
-    for c in z_copies + t_copies + list(y_copies.values()) + list(x_copies.values()) + list(d_copies.values()):
+
+    for c in z_copies + t_copies + list(copies.values()):
         c.wait_send()
 
     def sent(k, carry):
@@ -517,13 +605,13 @@
 
     lax.fori_loop(1, groups, sent, 0)
 
-    def sent_first(k, carry):
-        first_copy(k, 0).wait_send()
-        first_copy(k, 1).wait_send()
+    def sent_first(i, carry):
+        first_copy(i).wait_send()
+        put(i).wait()
         return carry
 
-    lax.fori_loop(1, 8, sent_first, 0)
-    first_copy(0, 1 - cb).wait_send()
+    lax.fori_loop(1, 16, sent_first, 0)
+    put(0).wait()
     col_copy.wait_send()
     pl.when(s > 0)(to_above.wait_send)
     pl.when(s < 15)(to_below.wait_send)
@@ -543,7 +631,7 @@
             out[part, :, side * half : (side + 1) * half] = jnp.swapaxes(jnp.concatenate(lines, axis=0), 0, 1)
         return carry
 
-    lax.fori_loop(0, chans // 8, some, 0)
+    lax.fori_loop(0, chans // 8, some, 0, unroll=True)
 
 
 def body(spectrum, land_sea, courant, refract, depth_dx, depth_dy, w_in, w_out):
@@ -553,16 +641,24 @@
     angles = (np.arange(DIRS, dtype=np.float32) + np.float32(0.5)) * np.float32(2.0 * math.pi / DIRS)
     cos_table = np.ascontiguousarray(np.broadcast_to(np.tile(np.cos(angles), freqs)[:, None], (chans, cols)))
     sin_table = np.ascontiguousarray(np.broadcast_to(np.tile(np.sin(angles), freqs)[:, None], (chans, cols)))
-    vmem = pl.BlockSpec(memory_space=pltpu.VMEM)
+    anywhere = pl.BlockSpec(memory_space=pl.ANY)
     smem = pl.BlockSpec(memory_space=pltpu.SMEM)
     dma = pltpu.SemaphoreType.DMA
     i16, f32, b16 = jnp.int16, jnp.float32, jnp.bfloat16
     back = pl.pallas_call(
         kernel,
         out_shape=jax.ShapeDtypeStruct((16, 4, chans, half), i16),
-        in_specs=[vmem] * 4 + [smem] * 2 + [vmem] * 4,
-        out_specs=vmem,
+        in_specs=[anywhere] * 4 + [smem] * 2 + [anywhere] * 4,
+        out_specs=anywhere,
         scratch_shapes=[
+            pltpu.VMEM((chans, rows, cols), f32),
+            pltpu.VMEM((rows, cols), f32),
+            pltpu.VMEM((rows, cols), f32),
+            pltpu.VMEM((rows, cols), jnp.int32),
+            pltpu.VMEM((chans, cols), f32),
+            pltpu.VMEM((chans, cols), f32),
+            pltpu.VMEM((9, 128, 128), b16),
+            pltpu.VMEM((128, 9 * 128), b16),
             pltpu.VMEM((rows + 2, chans, cols), f32),
             pltpu.VMEM((8, cols), f32),
             pltpu.VMEM((9, 128, 128), b16),
@@ -578,13 +674,14 @@
             pltpu.VMEM((chans, half), f32),
             pltpu.VMEM((16, 6, chans, half), f32),
             pltpu.VMEM((16, chans, cols), f32),
-            pltpu.VMEM((16 * chans, cols), b16),
-            pltpu.VMEM((2048, cols), b16),
+            pltpu.VMEM((2, 16 * chans, cols), b16),
+            pltpu.VMEM((2, 2048, cols), b16),
             pltpu.VMEM((16 * chans, cols), f32),
             pltpu.VMEM((7, chans, cols), f32),
             dma((3,)), dma((3,)), dma((4,)), dma((4,)), dma((4, 4)), dma((4, 4)), dma((4, 4)), dma((4, 4)),
-            dma((8, 2)), dma((8, 2)), dma((16,)), dma((16,)), dma((2,)), dma((2,)), dma((2, 16)), dma((2, 16)),
-            dma((2,)), dma((2,)), dma((1,)), dma((1,)), dma((1,)),
+            dma((16,)), dma((16,)), dma((16,)), dma((16,)), dma((2,)), dma((2,)), dma((2, 16)), dma((2, 16)),
+            dma((2,)), dma((2,)), dma((1,)), dma((1,)), dma((4,)), dma((4,)), dma((4,)), dma((4,)),
+            dma((1,)), dma((8,)), dma((16,)),
         ],
         compiler_params=pltpu.CompilerParams(
             collective_id=0, has_side_effects=True, vmem_limit_bytes=60 * 1024 * 1024

time: 126 us -> 111 us (0.88)
  the two profiles are of different devices: /device:TPU:248 before, /device:TPU:1 now
where the time goes in v3:
time: 111 us; the launch traced here: 110 us
  Pallas kernels  110 us (99%)
    pallas_call x1, Pallas kernels, body(): pl.pallas_call(kernel, out_shape=jax.ShapeDtypeStruct((16, 4, chans, half...  106 us
    pallas_call x1, Pallas kernels, body(): pl.pallas_call(turn_back, grid=(4,), out_shape=jax.ShapeDtypeStruct((chan...  3.93 us

profile of v3, /device:TPU:1, one launch (start us, length us, event | category | flops | bytes accessed | tf_op | source)
XLA Modules:
  0.0 110.4 jit_solution(18087389630126901365)
XLA Ops:
  0.0 106.5 %shard_map.100 = s16[16,4,72,128]{3,2,1,0:T(8,128)(2,1)} custom-call(f32[72,32,256]{2,1,0:T(8,128)} %bitcast.5, f32[32,256]{1,0:T(8,128)} %dx_in.1, f32[32,256]{1,0:T(8,128)} %dy_in.1, s32[32,256]{1,0:T(8,128)} %land_in.1, f32[2]{0:T(128)} %courant.1, f32[2]{0:T(128)} %refract.1, f32[72,256]{1,0:T(8,128)} %constant.4.clone.cos_in, ...), custom_call_target="tpu_custom_call" | custom-call | tf_op jit(solution)/shard_map/pallas_call | solution.py:648
  106.5 3.9 %shard_map.101 = f32[72,32,256]{2,1,0:T(8,128)} custom-call(s16[8,2,4,72,128]{4,3,2,1,0:T(8,128)(2,1)} %bitcast.4), custom_call_target="tpu_custom_call" | custom-call | tf_op jit(solution)/shard_map/pallas_call | solution.py:693

commit v4 on v3

--- a/solution.py
+++ b/solution.py
@@ -33,14 +33,14 @@
 def freq_of(rb, cb):
     high = rb // 4
     yy = rb % 4
-    return (yy + high * (3 - 2 * yy)) * 4 + high * 2 + cb
+    return (yy + high * (3 - 2 * yy)) * 4 + high + cb * 2
 
 
 def block_of(f):
     y = f // 4
     zl = f % 4
-    high = zl // 2
-    return high * 4 + y + high * (3 - 2 * y), zl % 2
+    high = zl % 2
+    return high * 4 + y + high * (3 - 2 * y), zl // 2
 
 
 def coefficients(table, cosine, sine):
@@ -76,14 +76,16 @@
 
 
 def gelu(x):
-    return 0.5 * x * (1.0 + jnp.tanh(math.sqrt(2.0 / math.pi) * (x + 0.044715 * x * x * x)))
+    near = math.sqrt(2.0 / math.pi)
+    part = 0.5 * x
+    return part + part * jnp.tanh(x * (near + near * 0.044715 * (x * x)))
 
 
 def kernel(
     spectrum_in, dx_in, dy_in, land_in, courant, refract, cos_in, sin_in, w_in_in, w_out_in, out,
     spectrum, dx, dy, land, cos_ref, sin_ref, w_in, w_out,
     field, own_table, own_w, weights, codes1, got1, codes2, got2, table, edge_out, edge_in, col_out, col_in,
-    energy, moved, x_buf, h_buf, s_buf, coef_buf,
+    energy, moved, x_buf, h_buf, s_buf, coef_buf, coef_all,
     z_send, z_recv, y_send, y_recv, x_send, x_recv, d_send, d_recv, a_send, a_recv, t_send, t_recv,
     e_send, e_recv, b_send, b_recv, halo_send, halo_recv, c_send, c_recv, l_send, l_recv, m_send, m_recv,
     local_sem, load_sem, store_sem,
@@ -185,6 +187,10 @@
     def quarter(q):
         return pl.ds(pl.multiple_of(q * 32, 32), 32)
 
+    to_above = remote(field.at[1], field.at[rows + 1], halo_send.at[0], halo_recv.at[1], above)
+    to_below = remote(field.at[rows], field.at[0], halo_send.at[1], halo_recv.at[0], below)
+    pl.when(s > 0)(to_above.start)
+    pl.when(s < 15)(to_below.start)
     own_quarter = weights.at[core, f, :, quarter(x), :]
     z_copies = []
     for k in range(1, 4):
@@ -193,10 +199,6 @@
         )
         c.start()
         z_copies.append(c)
-    to_above = remote(field.at[1], field.at[rows + 1], halo_send.at[0], halo_recv.at[1], above)
-    to_below = remote(field.at[rows], field.at[0], halo_send.at[1], halo_recv.at[0], below)
-    pl.when(s > 0)(to_above.start)
-    pl.when(s < 15)(to_below.start)
     place = pltpu.make_async_copy(own_w.at[:, quarter(x), :], own_quarter, local_sem.at[0])
     place.start()
     table[f] = own_table[...]
@@ -217,9 +219,8 @@
     whole, front, rear = (0, 9), (0, 5), (5, 4)
     copies = {}
 
-    def by_quarter(b, q, ks=whole, count=None):
-        count = (4 if b == 0 else 3) if count is None else count
-        return weights.at[core, pl.ds(order[b] * 4, count), pl.ds(*ks), quarter(q), :]
+    def by_quarter(b, q, ks=whole):
+        return weights.at[core, pl.ds(order[b] * 4, 3), pl.ds(*ks), quarter(q), :]
 
     def by_piece(b, ks=whole):
         return weights.at[core, order[b] * 4 + 3, pl.ds(*ks)]
@@ -241,15 +242,41 @@
     def share(b, k):
         go(("d", b, k), by_quarter(b, xs[k]), d_send.at[b, k], d_recv.at[b, k], partner)
 
+    def last_quarter(q, ks=whole):
+        return weights.at[core, y * 4 + 3, pl.ds(*ks), quarter(q), :]
+
+    def share_last(k):
+        go(("d", 4, k), last_quarter(xs[k]), d_send.at[4, k], d_recv.at[4, k], partner)
+
+    def last_1():
+        block = last_quarter(x)
+        go(("x", 4, 0), block, x_send.at[4, 0], x_recv.at[4, 0], at_x(1))
+        go(("x", 4, 1), block, x_send.at[4, 1], x_recv.at[4, 1], at_x(3))
+        share_last(0)
+
+    def last_2():
+        got("x", 4, 0)
+        go(("x", 4, 2), last_quarter(xs[1], front), x_send.at[4, 2], x_recv.at[4, 2], at_x(1))
+        got("x", 4, 1)
+        go(("x", 4, 3), last_quarter(xs[2], rear), x_send.at[4, 3], x_recv.at[4, 3], at_x(3))
+        share_last(1)
+        share_last(2)
+
+    def last_3():
+        got("x", 4, 2)
+        got("x", 4, 3)
+        share_last(3)
+
     def share_piece(b):
         go(("m", b), by_piece(b), m_send.at[b], m_recv.at[b], partner)
 
     def weights_1():
         for c in z_copies:
             c.wait_recv()
-        own = by_quarter(0, x, count=3)
+        own = by_quarter(0, x)
         go(("y", 0), own, y_send.at[0], y_recv.at[0], y_right)
         go(("y", 1), own, y_send.at[1], y_recv.at[1], y_left)
+        last_1()
         spread(0)
 
     def weights_2():
@@ -301,35 +328,35 @@
     for i, c in enumerate(coef):
         coef_buf[i] = c
 
-    @pl.when(s > 0)
-    def _():
-        to_below.wait_recv()
-
-    @pl.when(s == 0)
-    def _():
-        field[0] = jnp.zeros((chans, cols), jnp.float32)
-
-    @pl.when(s < 15)
-    def _():
-        to_above.wait_recv()
-
-    @pl.when(s == 15)
-    def _():
-        field[rows + 1] = jnp.zeros((chans, cols), jnp.float32)
-
-    def first_rows(n):
-        def one(r, carry):
-            row = n * 4 + r
-            value = transport_row(
-                field[row], field[row + 1], field[row + 2], 0.0, 0.0, [coef_buf[i] for i in range(7)],
-                dx[pl.ds(row, 1), :], dy[pl.ds(row, 1), :], land[pl.ds(row, 1), :].astype(jnp.float32),
-            )
-            code = encode(value, TOP_T1)
-            codes1[n * 2, r] = code[:, :half]
-            codes1[n * 2 + 1, r] = code[:, half:]
-            return carry
-
-        lax.fori_loop(0, 4, one, 0)
+    def first_row(row, carry):
+        value = transport_row(
+            field[row], field[row + 1], field[row + 2], 0.0, 0.0, [coef_buf[i] for i in range(7)],
+            dx[pl.ds(row, 1), :], dy[pl.ds(row, 1), :], land[pl.ds(row, 1), :].astype(jnp.float32),
+        )
+        code = encode(value, TOP_T1)
+        n, r = row // 4, row % 4
+        codes1[n * 2, r] = code[:, :half]
+        codes1[n * 2 + 1, r] = code[:, half:]
+        return carry
+
+    def outer_rows():
+        @pl.when(s > 0)
+        def _():
+            to_below.wait_recv()
+
+        @pl.when(s == 0)
+        def _():
+            field[0] = jnp.zeros((chans, cols), jnp.float32)
+
+        @pl.when(s < 15)
+        def _():
+            to_above.wait_recv()
+
+        @pl.when(s == 15)
+        def _():
+            field[rows + 1] = jnp.zeros((chans, cols), jnp.float32)
+
+        lax.fori_loop(0, 2, lambda n, carry: first_row(n * (rows - 1), carry), 0)
 
     def first_copy(i):
         ky, kz = i // 4, i % 4
@@ -346,26 +373,37 @@
         remote(codes1.at[0], got1.at[g], a_send.at[i], a_recv.at[i], at_freq(g)).wait_recv()
         return carry
 
-    def all_rows(n, carry):
-        first_rows(n)
-        return carry
-
-    lax.fori_loop(0, 8, all_rows, 0)
+    lax.fori_loop(1, 16, first_row, 0)
+    weights_1()
+    lax.fori_loop(16, rows - 1, first_row, 0)
+    outer_rows()
     mine = pltpu.make_async_copy(codes1.at[rb * 2 + cb], got1.at[f], local_sem.at[0])
     mine.start()
-    weights_1()
-    lax.fori_loop(1, 4, first_send, 0)
+    lax.fori_loop(1, 8, first_send, 0)
+    lax.fori_loop(12, 16, first_send, 0)
+    last_2()
     weights_2()
+    weights_3()
     weights_5(0)
-    weights_3()
-    lax.fori_loop(4, 16, first_send, 0)
+    last_3()
+    pieces_1()
+    lax.fori_loop(8, 12, first_send, 0)
     mine.wait()
     weights_4()
-    weights_6(0)
-    pieces_1()
+    for k in range(1, groups):
+        t_copies[k - 1].wait_recv()
+
+    def all_coefficients(g, carry):
+        for i, c in enumerate(coefficients(table[g][:, :half], cos_ref[:, :half], sin_ref[:, :half])):
+            coef_all[g, i] = c
+        return carry
+
+    lax.fori_loop(0, groups, all_coefficients, 0)
     weights_5(1)
     weights_5(2)
     pieces_2()
+    weights_6(0)
+    weights_5(3)
 
     def rows_of(hidden, blocks, size):
         for n, at in enumerate(blocks):
@@ -422,6 +460,8 @@
     zeros = jnp.zeros((chans, cols), jnp.float32)
     thin = zeros[:, :half]
     lane = lax.broadcasted_iota(jnp.int32, (chans, half), 1)
+    edge_lane = (half - 1) * (1 - cb)
+    col_copies = [remote(col_out.at[p], col_in.at[p], c_send.at[p], c_recv.at[p], beside) for p in range(2)]
 
     edge_copies = [
         remote(edge_out.at[0], edge_in.at[1], e_send.at[0], e_recv.at[1], up),
@@ -453,14 +493,14 @@
         lax.fori_loop(0, 2, one, 0)
 
     first_layer_of(0)
-    weights_5(3)
     pieces_3()
     first_layer_of(1)
     weights_6(1)
-    first_layer_of(2)
     weights_6(2)
     weights_6(3)
-    first_layer_of(3)
+    first_layer_of(2)
+    for k in range(4):
+        got("d", 4, k)
     for b in range(1, 4):
         got("m", b)
 
@@ -469,6 +509,7 @@
         return carry
 
     lax.fori_loop(0, 2, last_one, 0)
+    first_layer_of(3)
     for p, (first, last) in enumerate(pairs):
         second_layer(p)
 
@@ -476,38 +517,34 @@
             value = both_of(g, pairs[p]) * growth(g)
             energy[g, first + 1] = value[:, :half]
             energy[g, last + 1] = value[:, half:]
-            if first == 0:
+            if p == 0:
                 code = encode(value, TOP_E1)
                 edge_out[0, g] = code[:, :half]
                 edge_out[1, g] = code[:, half:]
             return carry
 
-        lax.fori_loop(0, groups, update, 0)
-        if first == 0:
+        lax.fori_loop(0, groups, update, 0, unroll=2)
+        if p == 0:
             pl.when(has_up)(edge_copies[0].start)
             pl.when(has_down)(edge_copies[1].start)
 
-    edge_lane = (half - 1) * (1 - cb)
-
-    def pack(g, block):
-        for r in range(4):
-            at = g * 4 + r
-            turned = pltpu.roll(energy[g, r + 1], (at - edge_lane + half) % half, 1)
-            block = jnp.where(lane == at, turned, block)
-        return block
-
-    col_out[...] = lax.fori_loop(0, groups, pack, thin, unroll=4)
-    col_copy = remote(col_out, col_in, c_send.at[0], c_recv.at[0], beside)
-    col_copy.start()
-    for k in range(1, groups):
-        t_copies[k - 1].wait_recv()
+    for p in (1, 0):
+
+        def pack(g, block):
+            for i in range(2):
+                at = g * 2 + i
+                turned = pltpu.roll(energy[g, pairs[p][i] + 1], (at - edge_lane + half) % half, 1)
+                block = jnp.where(lane == at, turned, block)
+            return block
+
+        col_out[p] = lax.fori_loop(0, groups, pack, thin, unroll=4)
+        col_copies[p].start()
+
     west_side = cb.astype(jnp.float32)
-    land_lane = (half - 1) * (1 - cb)
 
     def my_half(line):
         return jnp.where(cb == 0, line[:, :half], line[:, half:])
 
-    col_copy.wait_recv()
 
     def fill(present, copy, slot, row):
         @pl.when(present)
@@ -528,17 +565,18 @@
 
             lax.fori_loop(0, groups, some, 0)
 
-    for n, pair in enumerate(((1, 2), (0, 3))):
+    for n, pair in enumerate(pairs[::-1]):
+        col_copies[1 - n].wait_recv()
         if n == 1:
             fill(has_up, edge_copies[1], 0, 0)
             fill(has_down, edge_copies[0], 1, 5)
 
         def second(g, total):
-            coef = coefficients(table[g][:, :half], cos_ref[:, :half], sin_ref[:, :half])
+            coef = [coef_all[g, i] for i in range(7)]
             done = []
-            for r in pair:
+            for i, r in enumerate(pair):
                 row = pl.ds(rb * 4 + r, 1)
-                side = pltpu.roll(col_in[...], (land_lane - (g * 4 + r) + half) % half, 1)
+                side = pltpu.roll(col_in[1 - n], (edge_lane - (g * 2 + i) + half) % half, 1)
                 done.append(
                     transport_row(
                         energy[g, r], energy[g, r + 1], energy[g, r + 2], side * west_side, side * (1.0 - west_side),
@@ -549,7 +587,7 @@
             moved[g] = value
             return total + value
 
-        scale_into_x(lax.fori_loop(0, groups, second, zeros), n)
+        scale_into_x(lax.fori_loop(0, groups, second, zeros, unroll=2), n)
 
         def quarters(q, carry):
             first_quarter(q, n)
@@ -572,7 +610,7 @@
             remote(codes2.at[g, two], got2.at[rb * 2 + cb, two], b_send.at[n, k], b_recv.at[n, k], at_freq(g)).start()
             return carry
 
-        lax.fori_loop(1, groups, finish_and_send, 0)
+        lax.fori_loop(1, groups, finish_and_send, 0, unroll=3)
         finish(0)
 
     own_back = pltpu.make_async_copy(codes2.at[f], got2.at[rb * 2 + cb], local_sem.at[0])
@@ -612,7 +650,8 @@
 
     lax.fori_loop(1, 16, sent_first, 0)
     put(0).wait()
-    col_copy.wait_send()
+    for c in col_copies:
+        c.wait_send()
     pl.when(s > 0)(to_above.wait_send)
     pl.when(s < 15)(to_below.wait_send)
     pl.when(has_up)(edge_copies[0].wait_send)
@@ -624,14 +663,18 @@
     half = codes.shape[-1]
     slot = (2, 0, 1, 3)
 
-    def some(c, carry):
-        part = pl.ds(pl.multiple_of(c * 8, 8), 8)
-        for side in range(2):
-            lines = [decode(codes[n, side, slot[r], part, :], TOP_E2)[None] for n in range(2) for r in range(4)]
-            out[part, :, side * half : (side + 1) * half] = jnp.swapaxes(jnp.concatenate(lines, axis=0), 0, 1)
-        return carry
-
-    lax.fori_loop(0, chans // 8, some, 0, unroll=True)
+    def some(i, carry):
+        lines_of = pl.ds(pl.multiple_of(i * 8, 8), 8)
+        for c in range(chans // 8):
+            part = pl.ds(c * 8, 8)
+            for side in range(2):
+                lines = [
+                    decode(codes[i * 2 + n, side, slot[r], part, :], TOP_E2)[None] for n in range(2) for r in range(4)
+                ]
+                out[part, lines_of, side * half : (side + 1) * half] = jnp.swapaxes(jnp.concatenate(lines, axis=0), 0, 1)
+        return carry
+
+    lax.fori_loop(0, 4, some, 0)
 
 
 def body(spectrum, land_sea, courant, refract, depth_dx, depth_dy, w_in, w_out):
@@ -670,17 +713,18 @@
             pltpu.VMEM((16, 8, cols), f32),
             pltpu.VMEM((2, 16, chans, half), i16),
             pltpu.VMEM((2, 16, chans, half), i16),
-            pltpu.VMEM((chans, half), f32),
-            pltpu.VMEM((chans, half), f32),
+            pltpu.VMEM((2, chans, half), f32),
+            pltpu.VMEM((2, chans, half), f32),
             pltpu.VMEM((16, 6, chans, half), f32),
             pltpu.VMEM((16, chans, cols), f32),
             pltpu.VMEM((2, 16 * chans, cols), b16),
             pltpu.VMEM((2, 2048, cols), b16),
             pltpu.VMEM((16 * chans, cols), f32),
             pltpu.VMEM((7, chans, cols), f32),
-            dma((3,)), dma((3,)), dma((4,)), dma((4,)), dma((4, 4)), dma((4, 4)), dma((4, 4)), dma((4, 4)),
+            pltpu.VMEM((16, 7, chans, half), f32),
+            dma((3,)), dma((3,)), dma((4,)), dma((4,)), dma((5, 4)), dma((5, 4)), dma((5, 4)), dma((5, 4)),
             dma((16,)), dma((16,)), dma((16,)), dma((16,)), dma((2,)), dma((2,)), dma((2, 16)), dma((2, 16)),
-            dma((2,)), dma((2,)), dma((1,)), dma((1,)), dma((4,)), dma((4,)), dma((4,)), dma((4,)),
+            dma((2,)), dma((2,)), dma((2,)), dma((2,)), dma((4,)), dma((4,)), dma((4,)), dma((4,)),
             dma((1,)), dma((8,)), dma((16,)),
         ],
         compiler_params=pltpu.CompilerParams(
@@ -692,10 +736,7 @@
     )
     result = pl.pallas_call(
         turn_back,
-        grid=(4,),
         out_shape=jax.ShapeDtypeStruct((chans, rows, cols), f32),
-        in_specs=[pl.BlockSpec((2, 2, 4, chans, half), lambda i: (i, 0, 0, 0, 0))],
-        out_specs=pl.BlockSpec((chans, 8, cols), lambda i: (0, i, 0)),
     )(back.reshape(8, 2, 4, chans, half))
     return result.reshape(freqs, dirs, rows, cols)
 

time: 111 us -> 104 us (0.937)
  Pallas kernels: 110 us -> 104 us
    pallas_call x1, Pallas kernels: 106 us -> 101 us  [body(): pl.pallas_call(kernel, out_shape=jax.ShapeDtypeStruct((16, 4, chans, half...]
where the time goes in v4:
time: 104 us
  Pallas kernels  104 us (100%)
    pallas_call x1, Pallas kernels, body(): pl.pallas_call(kernel, out_shape=jax.ShapeDtypeStruct((16, 4, chans, half...  101 us
    pallas_call x1, Pallas kernels, body(): pl.pallas_call(turn_back, out_shape=jax.ShapeDtypeStruct((chans, rows, co...  3.39 us

profile of v4, /device:TPU:1, one launch (start us, length us, event | category | flops | bytes accessed | tf_op | source)
XLA Modules:
  0.0 104.0 jit_solution(17894716179912866235)
XLA Ops:
  0.0 100.6 %shard_map.100 = s16[16,4,72,128]{3,2,1,0:T(8,128)(2,1)} custom-call(f32[72,32,256]{2,1,0:T(8,128)} %bitcast.5, f32[32,256]{1,0:T(8,128)} %dx_in.1, f32[32,256]{1,0:T(8,128)} %dy_in.1, s32[32,256]{1,0:T(8,128)} %land_in.1, f32[2]{0:T(128)} %courant.1, f32[2]{0:T(128)} %refract.1, f32[72,256]{1,0:T(8,128)} %constant.4.clone.cos_in, ...), custom_call_target="tpu_custom_call" | custom-call | tf_op jit(solution)/shard_map/pallas_call | solution.py:691
  100.6 3.4 %shard_map.101 = f32[72,32,256]{2,1,0:T(8,128)} custom-call(s16[8,2,4,72,128]{4,3,2,1,0:T(8,128)(2,1)} %bitcast.4), custom_call_target="tpu_custom_call" | custom-call | tf_op jit(solution)/shard_map/pallas_call | solution.py:737

commit v5 on v4

--- a/solution.py
+++ b/solution.py
@@ -108,6 +108,10 @@
     def at_x(step):
         return {"space": base + ((x + step) % 4) * 2 + core, "freq": f}
 
+    def at_z(step):
+        z = ((s // 8) * 4 + zl + step + 8) % 8
+        return {"space": (z // 4) * 8 + s % 8, "freq": y * 4 + z % 4}
+
     partner = {"space": s + 1 - 2 * core, "freq": f}
     above = {"space": jnp.maximum(s - 1, 0), "freq": f}
     below = {"space": jnp.minimum(s + 1, 15), "freq": f}
@@ -127,6 +131,8 @@
     greet(at_x(1))
     greet(at_x(3))
     greet(partner)
+    for step in (1, -1, 2, -2):
+        greet(at_z(step))
     over_top = jnp.logical_and(rb == 0, s > 0)
     over_bottom = jnp.logical_and(rb == 7, s < 15)
     other_above = jnp.logical_and(core == 0, s > 0)
@@ -177,7 +183,7 @@
     turn(0)
     turn(3)
     known = (over_top, over_bottom, other_above, other_below)
-    pl.semaphore_wait(barrier, 18 + sum(k.astype(jnp.int32) for k in known))
+    pl.semaphore_wait(barrier, 22 + sum(k.astype(jnp.int32) for k in known))
 
     def remote(src, dst, send, recv, target):
         return pltpu.make_async_remote_copy(
@@ -193,9 +199,10 @@
     pl.when(s < 15)(to_below.start)
     own_quarter = weights.at[core, f, :, quarter(x), :]
     z_copies = []
-    for k in range(1, 4):
+    for n, (step, ks) in enumerate(((1, (0, 9)), (-1, (0, 9)), (2, (0, 5)), (-2, (5, 4)))):
         c = remote(
-            own_w.at[:, quarter(x), :], own_quarter, z_send.at[k - 1], z_recv.at[k - 1], at_freq(y * 4 + (zl + k) % 4)
+            own_w.at[pl.ds(*ks), quarter(x), :], weights.at[core, f, pl.ds(*ks), quarter(x), :],
+            z_send.at[n], z_recv.at[n], at_z(step),
         )
         c.start()
         z_copies.append(c)
@@ -427,18 +434,22 @@
         for where, part in rows_of(hidden, [g * 128 for g in pieces], 128):
             h_buf[p, where, :] = part
 
-    def second_layer(p):
+    def first_half(i, p):
+        lhs = jnp.concatenate(
+            [jnp.concatenate([weights[0, i * 8 + n, k] for k in range(9)], axis=1) for n in range(8)], axis=0
+        )
+        hidden = gelu(jnp.dot(lhs, x_buf[p], preferred_element_type=jnp.float32)).astype(jnp.bfloat16)
+        h_buf[p, pl.ds(pl.multiple_of(i * 1024, 1024), 1024), :] = hidden
+
+    def second_part(first, count, p):
+        lhs = jnp.concatenate(
+            [jnp.concatenate([weights[1, g, first + k] for g in range(16)], axis=1) for k in range(count)], axis=0
+        )
+        return jnp.dot(lhs, h_buf[p], preferred_element_type=jnp.float32)
+
+    def second_by_parts(p):
         def some(i, carry):
-            lhs = jnp.concatenate(
-                [
-                    jnp.concatenate([weights[1, g, i * 3 + k] for g in range(16)], axis=1)
-                    for k in range(3)
-                ],
-                axis=0,
-            )
-            s_buf[pl.ds(pl.multiple_of(i * 384, 384), 384), :] = jnp.dot(
-                lhs, h_buf[p], preferred_element_type=jnp.float32
-            )
+            s_buf[pl.ds(pl.multiple_of(i * 384, 384), 384), :] = second_part(i * 3, 3, p)
             return carry
 
         lax.fori_loop(0, 3, some, 0)
@@ -463,10 +474,19 @@
     edge_lane = (half - 1) * (1 - cb)
     col_copies = [remote(col_out.at[p], col_in.at[p], c_send.at[p], c_recv.at[p], beside) for p in range(2)]
 
-    edge_copies = [
-        remote(edge_out.at[0], edge_in.at[1], e_send.at[0], e_recv.at[1], up),
-        remote(edge_out.at[1], edge_in.at[0], e_send.at[1], e_recv.at[0], down),
-    ]
+    def edge_copy(side, part):
+        some = pl.ds(part * 4, 4 + part * 8)
+        return remote(
+            edge_out.at[side, some], edge_in.at[1 - side, some], e_send.at[side, part], e_recv.at[1 - side, part],
+            up if side == 0 else down,
+        )
+
+    edge_copies = [[edge_copy(side, part) for part in range(2)] for side in range(2)]
+
+    def send_edges(part):
+        pl.when(has_up)(edge_copies[0][part].start)
+        pl.when(has_down)(edge_copies[1][part].start)
+
     lax.fori_loop(1, 16, first_arrival, 0)
     pairs = ((0, 3), (1, 2))
 
@@ -511,7 +531,7 @@
     lax.fori_loop(0, 2, last_one, 0)
     first_layer_of(3)
     for p, (first, last) in enumerate(pairs):
-        second_layer(p)
+        second_by_parts(p)
 
         def update(g, carry):
             value = both_of(g, pairs[p]) * growth(g)
@@ -525,8 +545,7 @@
 
         lax.fori_loop(0, groups, update, 0, unroll=2)
         if p == 0:
-            pl.when(has_up)(edge_copies[0].start)
-            pl.when(has_down)(edge_copies[1].start)
+            send_edges(0)
 
     for p in (1, 0):
 
@@ -539,6 +558,8 @@
 
         col_out[p] = lax.fori_loop(0, groups, pack, thin, unroll=4)
         col_copies[p].start()
+        if p == 1:
+            send_edges(1)
 
     west_side = cb.astype(jnp.float32)
 
@@ -546,10 +567,11 @@
         return jnp.where(cb == 0, line[:, :half], line[:, half:])
 
 
-    def fill(present, copy, slot, row):
+    def fill(present, copies_in, slot, row):
         @pl.when(present)
         def _():
-            copy.wait_recv()
+            for c in copies_in:
+                c.wait_recv()
 
             def some(g, carry):
                 energy[g, row] = decode(edge_in[slot, g], TOP_E1)
@@ -589,13 +611,12 @@
 
         scale_into_x(lax.fori_loop(0, groups, second, zeros, unroll=2), n)
 
-        def quarters(q, carry):
-            first_quarter(q, n)
+        def halves(i, carry):
+            first_half(i, n)
             return carry
 
-        lax.fori_loop(0, 4, quarters, 0)
-        first_rest(n)
-        second_layer(n)
+        lax.fori_loop(0, 2, halves, 0)
+        s_buf[...] = second_part(0, 9, n)
 
         def finish(k):
             g = (f + k) % 16
@@ -654,8 +675,9 @@
         c.wait_send()
     pl.when(s > 0)(to_above.wait_send)
     pl.when(s < 15)(to_below.wait_send)
-    pl.when(has_up)(edge_copies[0].wait_send)
-    pl.when(has_down)(edge_copies[1].wait_send)
+    for part in range(2):
+        pl.when(has_up)(edge_copies[0][part].wait_send)
+        pl.when(has_down)(edge_copies[1][part].wait_send)
 
 
 def turn_back(codes, out):
@@ -722,8 +744,8 @@
             pltpu.VMEM((16 * chans, cols), f32),
             pltpu.VMEM((7, chans, cols), f32),
             pltpu.VMEM((16, 7, chans, half), f32),
-            dma((3,)), dma((3,)), dma((4,)), dma((4,)), dma((5, 4)), dma((5, 4)), dma((5, 4)), dma((5, 4)),
-            dma((16,)), dma((16,)), dma((16,)), dma((16,)), dma((2,)), dma((2,)), dma((2, 16)), dma((2, 16)),
+            dma((4,)), dma((4,)), dma((4,)), dma((4,)), dma((5, 4)), dma((5, 4)), dma((5, 4)), dma((5, 4)),
+            dma((16,)), dma((16,)), dma((16,)), dma((16,)), dma((2, 2)), dma((2, 2)), dma((2, 16)), dma((2, 16)),
             dma((2,)), dma((2,)), dma((2,)), dma((2,)), dma((4,)), dma((4,)), dma((4,)), dma((4,)),
             dma((1,)), dma((8,)), dma((16,)),
         ],

time: 104 us -> 102 us (0.981)
  Pallas kernels: 104 us -> 102 us
    pallas_call x1, Pallas kernels: 101 us -> 98.7 us  [body(): pl.pallas_call(kernel, out_shape=jax.ShapeDtypeStruct((16, 4, chans, half...]
where the time goes in v5:
time: 102 us
  Pallas kernels  102 us (100%)
    pallas_call x1, Pallas kernels, body(): pl.pallas_call(kernel, out_shape=jax.ShapeDtypeStruct((16, 4, chans, half...  98.7 us
    pallas_call x1, Pallas kernels, body(): pl.pallas_call(turn_back, out_shape=jax.ShapeDtypeStruct((chans, rows, co...  3.39 us

profile of v5, /device:TPU:1, one launch (start us, length us, event | category | flops | bytes accessed | tf_op | source)
XLA Modules:
  0.0 102.1 jit_solution(17105254220659440722)
XLA Ops:
  0.0 98.7 %shard_map.100 = s16[16,4,72,128]{3,2,1,0:T(8,128)(2,1)} custom-call(f32[72,32,256]{2,1,0:T(8,128)} %bitcast.5, f32[32,256]{1,0:T(8,128)} %dx_in.1, f32[32,256]{1,0:T(8,128)} %dy_in.1, s32[32,256]{1,0:T(8,128)} %land_in.1, f32[2]{0:T(128)} %courant.1, f32[2]{0:T(128)} %refract.1, f32[72,256]{1,0:T(8,128)} %constant.4.clone.cos_in, ...), custom_call_target="tpu_custom_call" | custom-call | tf_op jit(solution)/shard_map/pallas_call | solution.py:713
  98.7 3.4 %shard_map.101 = f32[72,32,256]{2,1,0:T(8,128)} custom-call(s16[8,2,4,72,128]{4,3,2,1,0:T(8,128)(2,1)} %bitcast.4), custom_call_target="tpu_custom_call" | custom-call | tf_op jit(solution)/shard_map/pallas_call | solution.py:759

commit v6 on v5

--- a/solution.py
+++ b/solution.py
@@ -412,27 +412,19 @@
     weights_6(0)
     weights_5(3)
 
-    def rows_of(hidden, blocks, size):
-        for n, at in enumerate(blocks):
-            yield pl.ds(pl.multiple_of(at, size), size), hidden[n * size : (n + 1) * size]
-
-    def first_quarter(q, p):
+    def first_some(quarters, rest, p):
         pieces = [b * 4 + n for b in range(4) for n in range(3)]
+        parts = [(g, quarter(q), g * 128 + q * 32, 32) for q in quarters for g in pieces]
+        if rest:
+            parts += [(b * 4 + 3, pl.ds(0, 128), b * 512 + 384, 128) for b in range(4)]
         lhs = jnp.concatenate(
-            [jnp.concatenate([weights[0, g, k, quarter(q), :] for k in range(9)], axis=1) for g in pieces], axis=0
+            [jnp.concatenate([weights[0, g, k, some, :] for k in range(9)], axis=1) for g, some, _, _ in parts], axis=0
         )
         hidden = gelu(jnp.dot(lhs, x_buf[p], preferred_element_type=jnp.float32)).astype(jnp.bfloat16)
-        for where, part in rows_of(hidden, [g * 128 + q * 32 for g in pieces], 32):
-            h_buf[p, where, :] = part
-
-    def first_rest(p):
-        pieces = [b * 4 + 3 for b in range(4)]
-        lhs = jnp.concatenate(
-            [jnp.concatenate([weights[0, g, k] for k in range(9)], axis=1) for g in pieces], axis=0
-        )
-        hidden = gelu(jnp.dot(lhs, x_buf[p], preferred_element_type=jnp.float32)).astype(jnp.bfloat16)
-        for where, part in rows_of(hidden, [g * 128 for g in pieces], 128):
-            h_buf[p, where, :] = part
+        at = 0
+        for _, _, place_row, size in parts:
+            h_buf[p, pl.ds(pl.multiple_of(place_row, size), size), :] = hidden[at : at + size]
+            at += size
 
     def first_half(i, p):
         lhs = jnp.concatenate(
@@ -502,34 +494,29 @@
 
         scale_into_x(lax.fori_loop(0, groups, load, zeros), p)
 
-    def first_layer_of(i):
-        for b in range(4):
-            got("d", b, i)
+    def first_layer_of(which, rest):
+        for i in which:
+            for b in range(4):
+                got("d", b, i)
 
         def one(p, carry):
-            first_quarter(xs[i], p)
+            first_some([xs[i] for i in which], rest, p)
             return carry
 
         lax.fori_loop(0, 2, one, 0)
 
-    first_layer_of(0)
+    first_layer_of((0, 1), False)
     pieces_3()
-    first_layer_of(1)
     weights_6(1)
+    first_layer_of((2,), False)
     weights_6(2)
     weights_6(3)
-    first_layer_of(2)
     for k in range(4):
         got("d", 4, k)
     for b in range(1, 4):
         got("m", b)
-
-    def last_one(p, carry):
-        first_rest(p)
-        return carry
-
-    lax.fori_loop(0, 2, last_one, 0)
-    first_layer_of(3)
+    first_layer_of((), True)
+    first_layer_of((3,), False)
     for p, (first, last) in enumerate(pairs):
         second_by_parts(p)
 
@@ -680,23 +667,27 @@
         pl.when(has_down)(edge_copies[1][part].wait_send)
 
 
-def turn_back(codes, out):
+def turn_back(codes_in, out, codes, lines_out, in_sem, out_sem):
     chans = out.shape[0]
     half = codes.shape[-1]
     slot = (2, 0, 1, 3)
-
-    def some(i, carry):
-        lines_of = pl.ds(pl.multiple_of(i * 8, 8), 8)
+    come = [pltpu.make_async_copy(codes_in.at[pl.ds(i * 2, 2)], codes.at[i], in_sem.at[i]) for i in range(4)]
+    leave = [
+        pltpu.make_async_copy(lines_out.at[i], out.at[:, pl.ds(i * 8, 8), :], out_sem.at[i]) for i in range(4)
+    ]
+    for c in come:
+        c.start()
+    for i in range(4):
+        come[i].wait()
         for c in range(chans // 8):
             part = pl.ds(c * 8, 8)
             for side in range(2):
-                lines = [
-                    decode(codes[i * 2 + n, side, slot[r], part, :], TOP_E2)[None] for n in range(2) for r in range(4)
-                ]
-                out[part, lines_of, side * half : (side + 1) * half] = jnp.swapaxes(jnp.concatenate(lines, axis=0), 0, 1)
-        return carry
-
-    lax.fori_loop(0, 4, some, 0)
+                lines = [decode(codes[i, n, side, slot[r], part, :], TOP_E2)[None] for n in range(2) for r in range(4)]
+                turned = jnp.swapaxes(jnp.concatenate(lines, axis=0), 0, 1)
+                lines_out[i, part, :, side * half : (side + 1) * half] = turned
+        leave[i].start()
+    for c in leave:
+        c.wait()
 
 
 def body(spectrum, land_sea, courant, refract, depth_dx, depth_dy, w_in, w_out):
@@ -759,6 +750,14 @@
     result = pl.pallas_call(
         turn_back,
         out_shape=jax.ShapeDtypeStruct((chans, rows, cols), f32),
+        in_specs=[anywhere],
+        out_specs=anywhere,
+        scratch_shapes=[
+            pltpu.VMEM((4, 2, 2, 4, chans, half), i16),
+            pltpu.VMEM((4, chans, 8, cols), f32),
+            dma((4,)),
+            dma((4,)),
+        ],
     )(back.reshape(8, 2, 4, chans, half))
     return result.reshape(freqs, dirs, rows, cols)
 

time: 102 us -> 100 us (0.980)
  Pallas kernels: 102 us -> 100 us
    pallas_call x1, Pallas kernels: 98.7 us -> 97.6 us  [body(): pl.pallas_call(kernel, out_shape=jax.ShapeDtypeStruct((16, 4, chans, half...]
where the time goes in v6:
time: 100 us
  Pallas kernels  100 us (100%)
    pallas_call x1, Pallas kernels, body(): pl.pallas_call(kernel, out_shape=jax.ShapeDtypeStruct((16, 4, chans, half...  97.6 us
    pallas_call x1, Pallas kernels, body(): pl.pallas_call(turn_back, out_shape=jax.ShapeDtypeStruct((chans, rows, co...  2.6 us

profile of v6, /device:TPU:1, one launch (start us, length us, event | category | flops | bytes accessed | tf_op | source)
XLA Modules:
  0.0 100.2 jit_solution(2492192558078101377)
XLA Ops:
  0.0 97.6 %shard_map.100 = s16[16,4,72,128]{3,2,1,0:T(8,128)(2,1)} custom-call(f32[72,32,256]{2,1,0:T(8,128)} %bitcast.5, f32[32,256]{1,0:T(8,128)} %dx_in.1, f32[32,256]{1,0:T(8,128)} %dy_in.1, s32[32,256]{1,0:T(8,128)} %land_in.1, f32[2]{0:T(128)} %courant.1, f32[2]{0:T(128)} %refract.1, f32[72,256]{1,0:T(8,128)} %constant.4.clone.cos_in, ...), custom_call_target="tpu_custom_call" | custom-call | tf_op jit(solution)/shard_map/pallas_call | solution.py:704
  97.6 2.6 %shard_map.101 = f32[72,32,256]{2,1,0:T(8,128)} custom-call(s16[8,2,4,72,128]{4,3,2,1,0:T(8,128)(2,1)} %bitcast.4), custom_call_target="tpu_custom_call" | custom-call | tf_op jit(solution)/shard_map/pallas_call | solution.py:750
